TPU v7x, 256 devices: a whole 4x4x8 slice. The times are simulated.
256 devices in a mesh: section: 2 (over core), seq: 16 (over x, y), head: 8 (over z).
Axes of the slice: x: 4, y: 4, z: 8, core: 2. Of those that a mesh axis runs over, the one named last changes fastest.
Arguments:
- x_in: bfloat16 [2, 4096, 8192], P('section', 'seq', 'head'), may hold values from -6 to 6
- b_in: bfloat16 [2, 4096, 2048], P('section', 'seq', 'head'), may hold values from -6 to 6
- c_in: bfloat16 [2, 4096, 2048], P('section', 'seq', 'head'), may hold values from -6 to 6
- z_in: bfloat16 [2, 4096, 8192], P('section', 'seq', 'head'), may hold values from -6 to 6
- dt_raw: float32 [2, 128, 4096], P('section', 'head', 'seq'), may hold values from -5 to 5
- conv_x: float32 [2, 4, 8192], P('section', None, 'head'), may hold values from -3 to 3
- conv_b: float32 [2, 4, 2048], P('section', None, 'head'), may hold values from -3 to 3
- conv_c: float32 [2, 4, 2048], P('section', None, 'head'), may hold values from -3 to 3
- a_rate: float32 [2, 128], P('section', 'head'), may hold values from 0.0001 to 1
- dt_bias: float32 [2, 128], P('section', 'head'), may hold values from -3 to -0.5
- skip_d: float32 [2, 128], P('section', 'head'), may hold values from 0.5 to 2
- norm_gain: float32 [2, 8192], P('section', 'head'), may hold values from 0.25 to 1.75
- out_weight: bfloat16 [2, 8192, 8192], P('section', 'head', 'seq'), may hold values from -0.0625 to 0.0625
Outputs:
- mixed: bfloat16 [2, 4096, 8192], P('section', ('seq', 'head'))
All inputs are finite; a program needn't handle non-finite values.
Results may differ from a plain program's by a relative error of at most 0.007.
Values may be sent and summed in bfloat16 or wider, within the bound.
A program may use at most 128 MiB of HBM per device.

v0:
```python
import jax
import jax.numpy as jnp
from jax import lax
from jax.sharding import Mesh
from jax.sharding import PartitionSpec as P

N = 256
SEQ = ("seq_0", "seq_1")
SEQ_HEAD = ("seq_0", "seq_1", "head")


epsilon = 1e-05


def passed_along(block, axis, distance):
    devices = range(lax.axis_size(axis))
    route = [(i - distance, i) for i in devices if i - distance in devices]
    return lax.ppermute(block, axis, route)


def neutral_like(x, identity):
    return jax.tree.map(
        lambda part, zero: jnp.zeros_like(part) + jnp.asarray(zero, part.dtype), x, identity
    )


def entering(x, axes, combine, identity):
    before = start = neutral_like(x, identity)
    so_far = x
    for axis in reversed(axes):
        size, place = (lax.axis_size(axis), lax.axis_index(axis))
        pieces = jax.tree.map(lambda part: lax.all_gather(part, axis), so_far)
        inside, so_far = (start, start)
        for k in range(size):
            passed = k < place
            so_far = combine(so_far, jax.tree.map(lambda part: part[k], pieces))
            inside = jax.tree.map(lambda new, old: jnp.where(passed, new, old), so_far, inside)
        before = combine(inside, before)
    return before


def from_everyone(x, axis):
    size = lax.axis_size(axis)
    return lax.all_to_all(jnp.broadcast_to(x[None], (size, *x.shape)), axis, 0, 0, tiled=True)


def in_order(pieces, dim):
    pieces = jnp.moveaxis(pieces, 0, dim)
    shape = pieces.shape
    return pieces.reshape(*shape[:dim], shape[dim] * shape[dim + 1], *shape[dim + 2 :])


def collect(x, axis, dim):
    pieces = from_everyone(x, axis)
    return in_order(pieces, dim)


def passed_along_2(block, axis, distance):
    devices = range(lax.axis_size(axis))
    route = [((i - distance) % len(devices), i) for i in devices]
    return lax.ppermute(block, axis, route)


def conv_silu(padded, kernel, length):
    kernel_taps = kernel.shape[0]
    summed = jnp.zeros((length, padded.shape[1]), jnp.float32)
    for offset in range(kernel_taps):
        summed = summed + kernel[offset] * padded[offset : offset + length].astype(jnp.float32)
    return jax.nn.silu(summed).astype(jnp.bfloat16)


def carry_combine(earlier, latter):
    return (earlier[0] * latter[0], latter[0][:, :, None, None] * earlier[1] + latter[1])


def per_device(
    x_in,
    b_in,
    c_in,
    z_in,
    dt_raw,
    conv_x,
    conv_b,
    conv_c,
    a_rate,
    dt_bias,
    skip_d,
    norm_gain,
    out_weight,
):
    x_local = x_in[0]
    b_local = b_in[0]
    c_local = c_in[0]
    length = x_local.shape[0]
    kernel_taps = conv_x.shape[1]
    x_cols = x_local.shape[1]
    b_cols = b_local.shape[1]
    edge_rows = jnp.concatenate(
        [
            x_local[length - kernel_taps + 1 :],
            b_local[length - kernel_taps + 1 :],
            c_local[length - kernel_taps + 1 :],
        ],
        axis=1,
    )
    before = passed_along(edge_rows, SEQ, 1)
    x_conv = conv_silu(jnp.concatenate([before[:, :x_cols], x_local], axis=0), conv_x[0], length)
    b_conv = conv_silu(
        jnp.concatenate([before[:, x_cols : x_cols + b_cols], b_local], axis=0), conv_b[0], length
    )
    c_conv = conv_silu(
        jnp.concatenate([before[:, x_cols + b_cols :], c_local], axis=0), conv_c[0], length
    )
    head_count = dt_raw.shape[1]
    group_count = b_cols // N
    per_group = head_count // group_count
    head_dim = x_cols // head_count
    step_size = jax.nn.softplus(dt_raw[0] + dt_bias[0][:, None])
    log_decay = jnp.cumsum(-a_rate[0][:, None] * step_size, axis=1)
    x_groups = x_conv.reshape(length, group_count, per_group, head_dim)
    b_groups = b_conv.reshape(length, group_count, N)
    c_groups = c_conv.reshape(length, group_count, N)
    log_groups = log_decay.reshape(group_count, per_group, length)
    step_groups = step_size.reshape(group_count, per_group, length)
    scores = jnp.einsum("tgn,ugn->gtu", c_groups, b_groups, preferred_element_type=jnp.float32)
    causal = jnp.arange(length)[:, None] >= jnp.arange(length)[None, :]
    spread_log = log_groups[:, :, :, None] - log_groups[:, :, None, :]
    damping = jnp.where(causal, jnp.exp(jnp.minimum(spread_log, 0.0)), 0.0)
    weights = (damping * step_groups[:, :, None, :] * scores[:, None]).astype(jnp.bfloat16)
    inside = jnp.einsum("gjtu,ugjp->tgjp", weights, x_groups, preferred_element_type=jnp.float32)
    to_end = jnp.exp(log_groups[:, :, -1:] - log_groups) * step_groups
    x_weighted = (
        x_groups.astype(jnp.float32) * jnp.transpose(to_end, (2, 0, 1))[..., None]
    ).astype(jnp.bfloat16)
    block_sum = jnp.einsum(
        "ugjp,ugn->gjpn", x_weighted, b_groups, preferred_element_type=jnp.float32
    )
    block_decay = jnp.exp(log_groups[:, :, -1])
    identity = (jnp.ones_like(block_decay), jnp.zeros_like(block_sum))
    carried_decay, carried = entering((block_decay, block_sum), SEQ, carry_combine, identity)
    carried_b = carried.astype(jnp.bfloat16)
    outside = jnp.einsum("tgn,gjpn->tgjp", c_groups, carried_b, preferred_element_type=jnp.float32)
    outside = outside * jnp.transpose(jnp.exp(log_groups), (2, 0, 1))[..., None]
    skip_term = skip_d[0].reshape(group_count, per_group)
    out_ssm = inside + outside + skip_term[None, :, :, None] * x_groups.astype(jnp.float32)
    gate_act = jax.nn.silu(z_in[0].astype(jnp.float32)).reshape(
        length, group_count, per_group * head_dim
    )
    gated = out_ssm.reshape(length, group_count, per_group * head_dim) * gate_act
    inverse_rms = lax.rsqrt(jnp.mean(gated * gated, axis=2, keepdims=True) + epsilon)
    hidden = ((gated * inverse_rms).reshape(length, x_cols) * norm_gain[0]).astype(jnp.bfloat16)
    local_weight = out_weight[0]
    full_columns = lax.all_gather(local_weight, "head", axis=0, tiled=True)
    owned_rows = lax.all_to_all(hidden, "head", split_axis=0, concat_axis=1, tiled=True)
    column_block = jnp.dot(
        collect(owned_rows, SEQ, 0), full_columns, preferred_element_type=jnp.float32
    ).astype(jnp.bfloat16)
    mixed = lax.all_to_all(column_block, SEQ, split_axis=0, concat_axis=1, tiled=True)
    passed = passed_along_2(mixed, "section", 1)
    return passed[None]


def solution(mesh):
    finer = Mesh(
        mesh.devices.reshape(mesh.shape["section"], 4, 4, mesh.shape["head"]),
        ("section", "seq_0", "seq_1", "head"),
    )
    return jax.shard_map(
        per_device,
        mesh=finer,
        in_specs=(
            P("section", SEQ, "head"),
            P("section", SEQ, "head"),
            P("section", SEQ, "head"),
            P("section", SEQ, "head"),
            P("section", "head", SEQ),
            P("section", None, "head"),
            P("section", None, "head"),
            P("section", None, "head"),
            P("section", "head"),
            P("section", "head"),
            P("section", "head"),
            P("section", "head"),
            P("section", "head", SEQ),
        ),
        out_specs=P("section", SEQ_HEAD, None),
        check_vma=False,
    )
```

profile of v0, /device:TPU:1, one launch (start us, length us, event | category | flops | bytes accessed | tf_op | source)
XLA Modules:
  0.0 360.7 jit_solution(4623957862641445590)
XLA Ops:
  8.2 4.0 %collective-permute-start = (bf16[3,1536]{0,1:T(8,128)(2,1)S(1)}, bf16[3,1536]{0,1:T(8,128)(2,1)S(1)}, u32[]{:S(2)}, u32[]{:S(2)}) collective-permute-start(bf16[3,1536]{0,1:T(8,128)(2,1)S(1)} %copy.48), channel_id=1, source_target_pairs={{0,8},{8,16},{16,24},{24,32},{32,40},{40,48},{48,56},{56,64},{64,7... | collective-permute-start | bytes 27656 | tf_op jit(solution)/shard_map/ppermute | solution.py:18
  18.0 1.2 copy.49
  20.2 1.4 multiply_convert_fusion.6
  21.5 1.5 fusion.24
  23.0 1.3 fusion.50
  24.4 9.0 %all-gather = f32[4,16,1]{1,2,0:T(1,128)S(1)} all-gather(f32[1,16,1]{1,2,0:T(1,128)S(1)} %exp.90), channel_id=2, replica_groups=mesh['section'=2,'seq_0'=4,'seq_1'=4,'head'=8] {'seq_1'}, dimensions={0}, use_global_device_ids=true | all-gather | bytes 320 | tf_op jit(solution)/shard_map/all_gather | solution.py:32
  33.4 46.4 %all-gather.9.cloned.1.call-done = f32[64,64,256]{2,1,0:T(8,128)} async-done(((f32[16,64,256]{2,1,0:T(8,128)}), f32[64,64,256]{2,1,0:T(8,128)}) %all-gather.9.cloned.1.call-update) | async-done | bytes 4194320 | tf_op jit(solution)/shard_map/all_gather | solution.py:32
  79.8 3.6 %fusion.20 = f32[1,1,16,64,256]{4,3,2,1,0:T(8,128)} fusion(f32[64,64,256]{2,1,0:T(8,128)} %all-gather.9.cloned.1.call-done, f32[16]{0:T(128)S(1)} %get-tuple-element.31, f32[16]{0:T(128)S(1)} %get-tuple-element.30, f32[16]{0:T(128)S(1)} %get-tuple-element.24, f32[16]{0:T(128)S(1)} %get-tuple-element.32), kind=kLoop, calls=%fused_computation.25 | loop fusion | flops 1835008 | bytes 5243136 | tf_op jit(solution)/shard_map/add | solution.py:73
  84.5 1.1 convert_element_type.148
  85.6 7.6 %all_gather.22 = f32[4,1,16]{2,1,0:T(1,128)S(1)} all-gather(f32[1,1,16]{2,1,0:T(1,128)S(1)} %get-tuple-element.29), channel_id=1, replica_groups=mesh['section'=2,'seq_0'=4,'seq_1'=4,'head'=8] {'seq_0'}, dimensions={0}, use_global_device_ids=true | all-gather | bytes 320 | tf_op jit(solution)/shard_map/all_gather | solution.py:32
  94.0 2.5 fusion.9
  96.5 38.2 %all-gather.7.cloned.1.call-done = f32[4,1,16,64,256]{4,3,2,1,0:T(8,128)} async-done(((f32[1,1,16,64,256]{4,3,2,1,0:T(8,128)}), f32[4,1,16,64,256]{4,3,2,1,0:T(8,128)}) %all-gather.7.cloned.1.call-update) | async-done | bytes 4194320 | tf_op jit(solution)/shard_map/all_gather | solution.py:32
  134.7 5.7 %multiply_reduce_fusion = (f32[256]{0:T(256)S(1)}, f32[256,1,16,64]{0,3,2,1:T(8,128)}) fusion(f32[256,1,16,64]{0,3,2,1:T(8,128)S(1)} %bitcast.184, f32[16]{0:T(128)S(1)} %bitcast.209, f32[256,1,16,64]{0,3,2,1:T(8,128)} %fusion.9, f32[256,16]{0,1:T(8,128)S(1)} %get-tuple-element.9, bf16[256,256]{1,0:T(8,128)(2,1)S(1)} %multiply_convert_fusion.7, ...), kind=kOutput, calls=%fused_computation.35 | convolution fusion | flops 143392512 | bytes 12207688 | tf_op jit(solution)/shard_map/tgn,gjpn->tgjp/dot_general | solution.py:142
  140.4 2.5 copy.56
  143.6 1.6 multiply_convert_fusion.4
  145.2 29.7 %all_to_all.37 = bf16[8,32,1024]{2,1,0:T(8,128)(2,1)S(1)} all-to-all(bf16[8,32,1024]{2,1,0:T(8,128)(2,1)S(1)} %multiply_convert_fusion.4), channel_id=1, replica_groups=mesh['section'=2,'seq_0'=4,'seq_1'=4,'head'=8] {'head'}, dimensions={0} | all-to-all | bytes 1048576 | tf_op jit(solution)/shard_map/all_to_all | solution.py:154
  174.9 4.2 %broadcast_in_dim.36 = bf16[16,32,8192]{2,1,0:T(8,128)(2,1)} broadcast(bf16[32,8192]{1,0:T(8,128)(2,1)S(1)} %bitcast.181), dimensions={1,2} | broadcast | bytes 8912896 | tf_op jit(solution)/shard_map/broadcast_in_dim | solution.py:44
  179.2 5.7 %all-to-all-start.1 = ((bf16[16,32,8192]{2,1,0:T(8,128)(2,1)}), bf16[16,32,8192]{2,1,0:T(8,128)(2,1)}, u32[]{:S(2)}, u32[]{:S(2)}) async-start(bf16[16,32,8192]{2,1,0:T(8,128)(2,1)} %broadcast_in_dim.36), calls=%async_computation.1 | async-start | bytes 16777216 | tf_op jit(solution)/shard_map/all_to_all | solution.py:44
  184.8 57.4 %all-gather.11.cloned.1.call-done = bf16[1,8192,512]{2,1,0:T(8,128)(2,1)} async-done(((bf16[1,1024,512]{2,1,0:T(8,128)(2,1)}), bf16[1,8192,512]{2,1,0:T(8,128)(2,1)}) %all-gather.11.cloned.1.call-update) | async-done | bytes 8388624 | tf_op jit(solution)/shard_map/all_gather | solution.py:153
  242.2 74.1 %all-to-all-done.1 = bf16[16,32,8192]{2,1,0:T(8,128)(2,1)} async-done(((bf16[16,32,8192]{2,1,0:T(8,128)(2,1)}), bf16[16,32,8192]{2,1,0:T(8,128)(2,1)}, u32[]{:S(2)}, u32[]{:S(2)}) %all-to-all-start.1) | async-done | bytes 8388640 | tf_op jit(solution)/shard_map/all_to_all | solution.py:44
  316.4 10.2 %fusion.13 = bf16[512,512]{1,0:T(8,128)(2,1)S(1)} fusion(bf16[512,8192]{1,0:T(8,128)(2,1)} %bitcast.55, bf16[1,8192,512]{2,1,0:T(8,128)(2,1)} %all-gather.11.cloned.1.call-done), kind=kOutput, calls=%fused_computation.15 | convolution fusion | flops 4295229440 | bytes 17301504 | tf_op jit(solution)/shard_map/dot_general | solution.py:155
  326.6 19.9 %all_to_all.38 = bf16[16,32,512]{2,1,0:T(8,128)(2,1)S(1)} all-to-all(bf16[16,32,512]{2,1,0:T(8,128)(2,1)S(1)} %bitcast.189), channel_id=1, replica_groups=mesh['section'=2,'seq_0'=4,'seq_1'=4,'head'=8] {'seq_0','seq_1'}, dimensions={0} | all-to-all | bytes 1048576 | tf_op jit(solution)/shard_map/all_to_all | solution.py:158
  346.6 5.2 %collective-permute-start.1 = (bf16[32,8192]{1,0:T(8,128)(2,1)S(1)}, bf16[32,8192]{1,0:T(8,128)(2,1)S(1)}, u32[]{:S(2)}, u32[]{:S(2)}) collective-permute-start(bf16[32,8192]{1,0:T(8,128)(2,1)S(1)} %bitcast.187), channel_id=1, source_target_pairs={{128,0},{0,128},{129,1},{1,129},{130,2},{2,130},{131,3},{3,131},{1... | collective-permute-start | bytes 1572872 | tf_op jit(solution)/shard_map/ppermute | solution.py:61
  351.8 1.5 collective-permute-done.1
  (63 shorter events, 11.6 us)
Async XLA Ops:
  6.5 73.3 %all-gather.9.cloned.1.call-start = ((), (), s32[]{:S(2)}) async-start(), calls=%async_computation.4 | async-start | bytes 5242880 | tf_op jit(solution)/shard_map/all_gather | solution.py:32
  8.2 11.8 %collective-permute-start = (bf16[3,1536]{0,1:T(8,128)(2,1)S(1)}, bf16[3,1536]{0,1:T(8,128)(2,1)S(1)}, u32[]{:S(2)}, u32[]{:S(2)}) collective-permute-start(bf16[3,1536]{0,1:T(8,128)(2,1)S(1)} %copy.48), channel_id=1, source_target_pairs={{0,8},{8,16},{16,24},{24,32},{32,40},{40,48},{48,56},{56,64},{64,7... | collective-permute-start | bytes 27656 | tf_op jit(solution)/shard_map/ppermute | solution.py:18
  24.3 59.9 %copy-start.1 = (bf16[1,256,1024]{2,1,0:T(8,128)(2,1)S(1)}, bf16[1,256,1024]{2,1,0:T(8,128)(2,1)}, u32[]{:S(2)}) copy-start(bf16[1,256,1024]{2,1,0:T(8,128)(2,1)} %param.16) | copy-start | bytes 1572868
  24.3 110.4 %all-gather.7.cloned.1.call-start = ((), (), s32[]{:S(2)}) async-start(), calls=%async_computation.3 | async-start | bytes 5242880 | tf_op jit(solution)/shard_map/all_gather | solution.py:32
  79.8 13.4 %copy-start.6 = (f32[1,4,256]{2,1,0:T(4,128)S(1)}, f32[1,4,256]{2,1,0:T(4,128)}, u32[]{:S(2)}) copy-start(f32[1,4,256]{2,1,0:T(4,128)} %param.20) | copy-start | bytes 12292
  79.8 13.4 %copy-start.2 = (f32[1,16,256]{2,1,0:T(8,128)S(1)}, f32[1,16,256]{2,1,0:T(8,128)}, u32[]{:S(2)}) copy-start(f32[1,16,256]{2,1,0:T(8,128)} %param.17) | copy-start | bytes 49156
  79.8 13.4 %copy-start.4 = (f32[1,16]{1,0:T(1,128)S(1)}, f32[1,16]{1,0:T(1,128)}, u32[]{:S(2)}) copy-start(f32[1,16]{1,0:T(1,128)} %param.22) | copy-start | bytes 196
  79.8 13.7 %copy-start.3 = (bf16[1,256,256]{2,1,0:T(8,128)(2,1)S(1)}, bf16[1,256,256]{2,1,0:T(8,128)(2,1)}, u32[]{:S(2)}) copy-start(bf16[1,256,256]{2,1,0:T(8,128)(2,1)} %param.15) | copy-start | bytes 393220
  83.5 158.7 %all-gather.11.cloned.1.call-start = ((), (), s32[]{:S(2)}) async-start(), calls=%async_computation.5 | async-start | bytes 9437184 | tf_op jit(solution)/shard_map/all_gather | solution.py:153
  93.7 41.0 %copy-start = (f32[1,1,16,64,256]{4,3,2,1,0:T(8,128)S(1)}, f32[1,1,16,64,256]{4,3,2,1,0:T(8,128)}, u32[]{:S(2)}) copy-start(f32[1,1,16,64,256]{4,3,2,1,0:T(8,128)} %fusion.20) | copy-start | bytes 3145732
  93.7 41.0 %copy-start.7 = (f32[1,16]{1,0:T(1,128)S(1)}, f32[1,16]{1,0:T(1,128)}, u32[]{:S(2)}) copy-start(f32[1,16]{1,0:T(1,128)} %param.23) | copy-start | bytes 196
  140.4 3.2 copy-start.5
  179.2 137.2 %all-to-all-start.1 = ((bf16[16,32,8192]{2,1,0:T(8,128)(2,1)}), bf16[16,32,8192]{2,1,0:T(8,128)(2,1)}, u32[]{:S(2)}, u32[]{:S(2)}) async-start(bf16[16,32,8192]{2,1,0:T(8,128)(2,1)} %broadcast_in_dim.36), calls=%async_computation.1 | async-start | bytes 16777216 | tf_op jit(solution)/shard_map/all_to_all | solution.py:44
  346.6 6.7 %collective-permute-start.1 = (bf16[32,8192]{1,0:T(8,128)(2,1)S(1)}, bf16[32,8192]{1,0:T(8,128)(2,1)S(1)}, u32[]{:S(2)}, u32[]{:S(2)}) collective-permute-start(bf16[32,8192]{1,0:T(8,128)(2,1)S(1)} %bitcast.187), channel_id=1, source_target_pairs={{128,0},{0,128},{129,1},{1,129},{130,2},{2,130},{131,3},{3,131},{1... | collective-permute-start | bytes 1572872 | tf_op jit(solution)/shard_map/ppermute | solution.py:61
Sparse Core Ops, SparseCore 0:
  24.5 55.3 all-gather.8
  83.6 51.0 all-gather.6
  136.5 105.6 all-gather.10
where the time goes:
time: 361 us
  waiting for transfers between devices  219 us (61%)
  blocking collectives  66.2 us (18%)
  matrix products  19.9 us (6%)
  starting transfers between devices  15 us (4%)
  local copies, waits for them, and re-layouts  14.5 us (4%)
  between operations  13.4 us (4%)
  other arithmetic  12.5 us (3%)
    all_gather x2, waiting for transfers between devices, entering(): pieces = jax.tree.map(lambda part: lax.all_gather(part, axis), so_far)  84.7 us
    all_to_all x1, waiting for transfers between devices, from_everyone(): lax.all_to_all(jnp.broadcast_to(x[None], (size, *x.shape)), axis, 0, 0, t...  74.1 us
    all_gather x1, waiting for transfers between devices, per_device(): full_columns = lax.all_gather(local_weight, 'head', axis=0, tiled=True)  57.4 us
    all_to_all x1, blocking collectives, per_device(): lax.all_to_all(hidden, 'head', split_axis=0, concat_axis=1, tiled=True)  29.7 us
    all_to_all x1, blocking collectives, per_device(): lax.all_to_all(column_block, SEQ, split_axis=0, concat_axis=1, tiled=True)  19.9 us
    all_gather x2, blocking collectives, entering(): pieces = jax.tree.map(lambda part: lax.all_gather(part, axis), so_far)  16.6 us
    dot_general x1, matrix products, per_device(): jnp.dot(collect(owned_rows, SEQ, 0), full_columns, preferred_element_type...  10.2 us
  transfers between devices with their start and end apart: 6, of which 6 were waited for; matrix products, arithmetic and copies ran while one was open for 7% of the time, Pallas kernels for 0%

commit v1 on v0

--- a/solution.py
+++ b/solution.py
@@ -3,6 +3,8 @@
 from jax import lax
 from jax.sharding import Mesh
 from jax.sharding import PartitionSpec as P
+from jax.experimental import pallas as pl
+from jax.experimental.pallas import tpu as pltpu
 
 N = 256
 SEQ = ("seq_0", "seq_1")
@@ -39,26 +41,208 @@
     return before
 
 
-def from_everyone(x, axis):
-    size = lax.axis_size(axis)
-    return lax.all_to_all(jnp.broadcast_to(x[None], (size, *x.shape)), axis, 0, 0, tiled=True)
-
-
-def in_order(pieces, dim):
-    pieces = jnp.moveaxis(pieces, 0, dim)
-    shape = pieces.shape
-    return pieces.reshape(*shape[:dim], shape[dim] * shape[dim + 1], *shape[dim + 2 :])
-
-
-def collect(x, axis, dim):
-    pieces = from_everyone(x, axis)
-    return in_order(pieces, dim)
-
-
-def passed_along_2(block, axis, distance):
-    devices = range(lax.axis_size(axis))
-    route = [((i - distance) % len(devices), i) for i in devices]
-    return lax.ppermute(block, axis, route)
+MESH = pl.DeviceIdType.MESH
+PIECES = (4, 3, 5, 2, 6, 1, 7, 0)
+OFFSETS = (0, 3, 1, 2)
+
+
+def send(src, dst, send_sem, recv_sem, **to):
+    return pltpu.make_async_remote_copy(
+        src_ref=src, dst_ref=dst, send_sem=send_sem, recv_sem=recv_sem,
+        device_id=to, device_id_type=MESH,
+    )
+
+
+def greet(peers):
+    barrier = pltpu.get_barrier_semaphore()
+    for peer in peers:
+        pl.semaphore_signal(barrier, inc=1, device_id=peer, device_id_type=MESH)
+    return lambda: pl.semaphore_wait(barrier, len(peers))
+
+
+def project_kernel(
+    hid, w, out, wg, ag, first_out, first_in, ring_out, ring_in, done,
+    w_own, w_send, w_recv, a_send, a_recv, r_send, r_recv, o_send, o_recv,
+):
+    s, x, y, h = (lax.axis_index(a) for a in ("section", "seq_0", "seq_1", "head"))
+    xr, xl = lax.rem(x + 1, 4), lax.rem(x + 3, 4)
+    ys = [lax.rem(y + o, 4) for o in OFFSETS]
+    up, down = lax.rem(h + 1, 8), lax.rem(h + 7, 8)
+    sides = (up, down)
+    own = pltpu.make_async_copy(w, wg.at[0], w_own)
+    own.start()
+    ready = greet(
+        [{"seq_1": v} for v in ys[1:]] + [{"seq_0": xr}, {"seq_0": xl}]
+        + [{"head": up}, {"head": down}] + [{"section": 1 - s, "seq_1": v} for v in ys]
+    )
+    for p, k in enumerate(PIECES):
+        rows = pl.ds(pl.multiple_of(lax.rem(h + k, 8) * 32, 32), 32)
+        ag[p * 128 : p * 128 + 32, :] = hid[rows, :]
+    ready()
+
+    def a_direct(p):
+        rows = pl.ds(pl.multiple_of(lax.rem(h + PIECES[p], 8) * 32, 32), 32)
+        copies = [
+            send(hid.at[rows], ag.at[pl.ds(p * 128 + 32, 32)], a_send.at[p, 0], a_recv.at[p, 0], seq_1=ys[2]),
+            send(hid.at[rows], ag.at[pl.ds(p * 128 + 64, 32)], a_send.at[p, 1], a_recv.at[p, 1], seq_1=ys[1]),
+        ]
+        if p == 0:
+            copies.append(
+                send(hid.at[rows], ag.at[pl.ds(96, 32)], a_send.at[p, 2], a_recv.at[p, 2], seq_1=ys[3])
+            )
+        return copies
+
+    def a_forward(p):
+        return [
+            send(ag.at[pl.ds(p * 128 + 32, 16)], ag.at[pl.ds(p * 128 + 96, 16)], a_send.at[p, 2], a_recv.at[p, 2], seq_1=ys[2]),
+            send(ag.at[pl.ds(p * 128 + 80, 16)], ag.at[pl.ds(p * 128 + 112, 16)], a_send.at[p, 3], a_recv.at[p, 3], seq_1=ys[1]),
+        ]
+
+    started = []
+
+    def start(copies):
+        for c in copies:
+            c.start()
+        started.extend(copies)
+        return copies
+
+    direct = {p: a_direct(p) for p in range(8)}
+    passed = {p: a_forward(p) for p in range(1, 8)}
+    start(direct[0])
+    w_direct = start([
+        send(w, wg.at[1], w_send.at[0], w_recv.at[0], seq_0=xr),
+        send(w, wg.at[2], w_send.at[1], w_recv.at[1], seq_0=xl),
+    ])
+    start(direct[1])
+    start(direct[2])
+    own.wait()
+
+    def forward(p):
+        direct[p][0].wait_recv()
+        passed_now = passed[p]
+        start(passed_now[:1])
+        direct[p][1].wait_recv()
+        start(passed_now[1:])
+
+    def arrived(p):
+        for c in passed[p]:
+            c.wait_recv()
+
+    def ring(stage, j, side):
+        src, dst = (first_out, first_in) if stage == 0 else (ring_out, ring_in)
+        at = (side, j) if stage == 0 else (side, stage - 1, j)
+        axis = {"head": sides[side]}
+        return send(src.at[at], dst.at[at], r_send.at[side, stage, j], r_recv.at[side, stage, j], **axis)
+
+    for c in direct[0]:
+        c.wait_recv()
+
+    def first(j, _):
+        part = jnp.dot(ag[0:128, :], wg[j], preferred_element_type=jnp.float32)
+        first_out[0, j] = part[:, :256].astype(jnp.bfloat16)
+        first_out[1, j] = part[:, 256:].astype(jnp.bfloat16)
+        ring(0, j, 0).start()
+        ring(0, j, 1).start()
+        return 0
+
+    first(0, 0)
+    for c in w_direct:
+        c.wait_recv()
+    w_passed = start([
+        send(wg.at[1, pl.ds(0, 512)], wg.at[3, pl.ds(0, 512)], w_send.at[2], w_recv.at[2], seq_0=xr),
+        send(wg.at[2, pl.ds(512, 512)], wg.at[3, pl.ds(512, 512)], w_send.at[3], w_recv.at[3], seq_0=xl),
+    ])
+    lax.fori_loop(1, 3, first, 0)
+    for c in w_passed:
+        c.wait_recv()
+    first(3, 0)
+    forward(1)
+    forward(2)
+
+    for stage in (1, 2, 3):
+        p = 2 * stage - 1
+        start(direct[p + 2])
+        if stage < 3:
+            start(direct[p + 3])
+        arrived(p)
+        arrived(p + 1)
+
+        def middle(j, _):
+            part = jnp.dot(ag[p * 128 : p * 128 + 256, :], wg[j], preferred_element_type=jnp.float32)
+            for side in (0, 1):
+                mine = part[side * 128 : side * 128 + 128]
+                ring(stage - 1, j, side).wait_recv()
+                if stage == 1:
+                    got = first_in[side, j].astype(jnp.float32)
+                    if side == 0:
+                        ring_out[side, 0, j, :, :256] = (mine[:, :256] + got).astype(jnp.bfloat16)
+                        ring_out[side, 0, j, :, 256:] = mine[:, 256:].astype(jnp.bfloat16)
+                    else:
+                        ring_out[side, 0, j, :, :256] = mine[:, :256].astype(jnp.bfloat16)
+                        ring_out[side, 0, j, :, 256:] = (mine[:, 256:] + got).astype(jnp.bfloat16)
+                else:
+                    got = ring_in[side, stage - 2, j].astype(jnp.float32)
+                    ring_out[side, stage - 1, j] = (mine + got).astype(jnp.bfloat16)
+            ring(stage, j, 0).start()
+            ring(stage, j, 1).start()
+            return 0
+
+        lax.fori_loop(0, 4, middle, 0)
+        forward(p + 2)
+        if stage < 3:
+            forward(p + 3)
+
+    arrived(7)
+    results = []
+    for j in range(4):
+        part = jnp.dot(ag[896:1024, :], wg[j], preferred_element_type=jnp.float32)
+        for side in (0, 1):
+            ring(3, j, side).wait_recv()
+        total = part + ring_in[0, 2, j].astype(jnp.float32) + ring_in[1, 2, j].astype(jnp.float32)
+        done[j] = total.astype(jnp.bfloat16)
+        column = (lax.rem(x + OFFSETS[j], 4) * 4 + y) * 512
+        cols = pl.ds(pl.multiple_of(column, 512), 512)
+        for r in range(4):
+            results.append(
+                send(done.at[j, pl.ds(r * 32, 32)], out.at[:, cols], o_send.at[r, j], o_recv.at[r, j], section=1 - s, seq_1=ys[r])
+            )
+        for c in results[-4:]:
+            c.start()
+
+    for c in started:
+        c.wait_send()
+    for stage in range(4):
+
+        def drain(j, _):
+            ring(stage, j, 0).wait_send()
+            ring(stage, j, 1).wait_send()
+            return 0
+
+        lax.fori_loop(0, 4, drain, 0)
+    for c in results:
+        c.wait_send()
+        c.wait_recv()
+
+
+def project(hidden, weight):
+    dma = pltpu.SemaphoreType.DMA
+    vmem = lambda *shape: pltpu.VMEM(shape, jnp.bfloat16)
+    return pl.pallas_call(
+        project_kernel,
+        out_shape=jax.ShapeDtypeStruct((32, 8192), jnp.bfloat16),
+        in_specs=[pl.BlockSpec(memory_space=pltpu.VMEM), pl.BlockSpec(memory_space=pl.ANY)],
+        out_specs=pl.BlockSpec(memory_space=pl.ANY),
+        scratch_shapes=[
+            vmem(4, 1024, 512), vmem(1024, 1024),
+            vmem(2, 4, 128, 256), vmem(2, 4, 128, 256),
+            vmem(2, 3, 4, 128, 512), vmem(2, 3, 4, 128, 512), vmem(4, 128, 512),
+            dma, dma((4,)), dma((4,)), dma((8, 4)), dma((8, 4)),
+            dma((2, 4, 4)), dma((2, 4, 4)), dma((4, 4)), dma((4, 4)),
+        ],
+        compiler_params=pltpu.CompilerParams(
+            collective_id=0, has_side_effects=True, vmem_limit_bytes=48 * 2**20
+        ),
+    )(hidden, weight)
 
 
 def conv_silu(padded, kernel, length):
@@ -150,13 +334,7 @@
     inverse_rms = lax.rsqrt(jnp.mean(gated * gated, axis=2, keepdims=True) + epsilon)
     hidden = ((gated * inverse_rms).reshape(length, x_cols) * norm_gain[0]).astype(jnp.bfloat16)
     local_weight = out_weight[0]
-    full_columns = lax.all_gather(local_weight, "head", axis=0, tiled=True)
-    owned_rows = lax.all_to_all(hidden, "head", split_axis=0, concat_axis=1, tiled=True)
-    column_block = jnp.dot(
-        collect(owned_rows, SEQ, 0), full_columns, preferred_element_type=jnp.float32
-    ).astype(jnp.bfloat16)
-    mixed = lax.all_to_all(column_block, SEQ, split_axis=0, concat_axis=1, tiled=True)
-    passed = passed_along_2(mixed, "section", 1)
+    passed = project(hidden, local_weight)
     return passed[None]
 
 

time: 361 us -> 236 us (0.65)
  waiting for transfers between devices: 219 us -> 81.7 us
  Pallas kernels: 0 us -> 88.3 us
  blocking collectives: 66.2 us -> 15.2 us
  starting transfers between devices: 15 us -> 4.06 us
  matrix products: 19.9 us -> 11.2 us
    pallas_call x0 -> x1, Pallas kernels: none -> 88.3 us  [project(): pl.pallas_call(project_kernel, out_shape=jax.ShapeDtypeStruct((32, 8192),...]
    all_to_all x1 -> x0, waiting for transfers between devices: 74.1 us -> none  [from_everyone(): lax.all_to_all(jnp.broadcast_to(x[None], (size, *x.shape)), axis, 0, 0, t...]
    all_gather x1 -> x0, waiting for transfers between devices: 57.4 us -> none  [per_device(): full_columns = lax.all_gather(local_weight, 'head', axis=0, tiled=True)]
    all_to_all x2 -> x0, blocking collectives: 49.6 us -> none  [the longest x1 29.7 us: per_device(): lax.all_to_all(hidden, 'head', split_axis=0, concat_axis=1, tiled=True)]
    dot_general x1 -> x0, matrix products: 10.2 us -> none  [per_device(): jnp.dot(collect(owned_rows, SEQ, 0), full_columns, preferred_element_type...]
    all_to_all x1 -> x0, starting transfers between devices: 5.67 us -> none  [from_everyone(): lax.all_to_all(jnp.broadcast_to(x[None], (size, *x.shape)), axis, 0, 0, t...]
    ppermute x1 -> x0, starting transfers between devices: 5.19 us -> none  [passed_along_2(): return lax.ppermute(block, axis, route)]
    broadcast_in_dim x2 -> x0, local copies, waits for them, and re-layouts: 4.28 us -> none  [from_everyone(): jnp.broadcast_to(x[None], (size, *x.shape))]
  transfers between devices with their start and end apart: 6 -> 3, of which waited for: 6 -> 2; matrix products, arithmetic and copies ran while one was open for 7% -> 6% of each run, Pallas kernels for 0% -> 0%
where the time goes in v1:
time: 236 us; the launch traced here: 235 us
  Pallas kernels  88.3 us (37%)
  waiting for transfers between devices  81.7 us (35%)
  blocking collectives  15.2 us (6%)
  between operations  13.7 us (6%)
  matrix products  11.2 us (5%)
  local copies, waits for them, and re-layouts  10.9 us (5%)
  other arithmetic  10.2 us (4%)
  starting transfers between devices  4.06 us (2%)
    pallas_call x1, Pallas kernels, project(): pl.pallas_call(project_kernel, out_shape=jax.ShapeDtypeStruct((32, 8192),...  88.3 us
    all_gather x2, waiting for transfers between devices, entering(): pieces = jax.tree.map(lambda part: lax.all_gather(part, axis), so_far)  81.7 us
    all_gather x2, blocking collectives, entering(): pieces = jax.tree.map(lambda part: lax.all_gather(part, axis), so_far)  15.2 us
    dot_general x1, matrix products, per_device(): jnp.einsum('tgn,gjpn->tgjp', c_groups, carried_b, preferred_element_type=...  5.96 us
  transfers between devices with their start and end apart: 3, of which 2 were waited for; matrix products, arithmetic and copies ran while one was open for 6% of the time, Pallas kernels for 0%

profile of v1, /device:TPU:1, one launch (start us, length us, event | category | flops | bytes accessed | tf_op | source)
XLA Modules:
  0.0 235.3 jit_solution(13738917157205533612)
XLA Ops:
  6.5 0.8 slice_bitcast_fusion.4
  7.3 0.7 slice_bitcast_fusion.5
  8.0 4.0 %collective-permute-start = (bf16[3,1536]{1,0:T(4,128)(2,1)S(1)}, bf16[3,1536]{1,0:T(4,128)(2,1)S(1)}, u32[]{:S(2)}, u32[]{:S(2)}) collective-permute-start(bf16[3,1536]{1,0:T(4,128)(2,1)S(1)} %pad_maximum_fusion.3), channel_id=1, source_target_pairs={{0,8},{8,16},{16,24},{24,32},{32,40},{40,48},{48,56},{56,64},{64,7... | collective-permute-start | bytes 27656 | tf_op jit(solution)/shard_map/ppermute | solution.py:20
  12.1 0.7 negate_bitcast_fusion
  12.7 0.7 squeeze.21
  13.5 0.7 fusion.53
  15.3 0.9 fusion.59
  16.2 0.8 exponential_bitcast_fusion
  17.0 0.8 fusion.61
  18.3 2.7 %multiply_convert_fusion.4 = (bf16[256,1024]{1,0:T(8,128)(2,1)S(1)}, bf16[256,1024]{1,0:T(8,128)(2,1)S(1)}) fusion(f32[256,1024]{1,0:T(8,128)S(1)} %copy.46, bf16[256,1024]{1,0:T(8,128)(2,1)} %bitcast.183, f32[1024]{0:T(1024)S(1)} %bitcast.189, bf16[3,1024]{1,0:T(4,128)(2,1)S(1)} %slice.217, f32[1024]{0:T(1024)S(1)} %bitcast.190, f32[1024]{0:T(1024)S(1)} %bitcast.188, ...), kind=kLoop, calls=%fused_computation.38 | loop fusion | flops 7340032 | bytes 2643968 | tf_op jit(solution)/shard_map/convert_element_type | solution.py:318
  21.4 1.3 fusion.51
  22.8 7.5 %all-gather = f32[4,16,1]{1,2,0:T(1,128)S(1)} all-gather(f32[1,16,1]{1,2,0:T(1,128)S(1)} %exp.89), channel_id=2, replica_groups=mesh['section'=2,'seq_0'=4,'seq_1'=4,'head'=8] {'seq_1'}, dimensions={0}, use_global_device_ids=true | all-gather | bytes 320 | tf_op jit(solution)/shard_map/all_gather | solution.py:34
  30.4 46.1 %all-gather.7.cloned.1.call-done = f32[64,64,256]{2,1,0:T(8,128)} async-done(((f32[16,64,256]{2,1,0:T(8,128)}), f32[64,64,256]{2,1,0:T(8,128)}) %all-gather.7.cloned.1.call-update) | async-done | bytes 4194320 | tf_op jit(solution)/shard_map/all_gather | solution.py:34
  76.4 3.6 %fusion.15 = f32[1,1,16,64,256]{4,3,2,1,0:T(8,128)} fusion(f32[64,64,256]{2,1,0:T(8,128)} %all-gather.7.cloned.1.call-done, f32[16]{0:T(128)S(1)} %get-tuple-element.31, f32[16]{0:T(128)S(1)} %get-tuple-element.30, f32[16]{0:T(128)S(1)} %get-tuple-element.24, f32[16]{0:T(128)S(1)} %get-tuple-element.32), kind=kLoop, calls=%fused_computation.22 | loop fusion | flops 1835008 | bytes 5243136 | tf_op jit(solution)/shard_map/add | solution.py:257
  80.1 1.2 copy.50
  81.3 7.6 %all_gather.19 = f32[4,1,16]{2,1,0:T(1,128)S(1)} all-gather(f32[1,1,16]{2,1,0:T(1,128)S(1)} %get-tuple-element.29), channel_id=1, replica_groups=mesh['section'=2,'seq_0'=4,'seq_1'=4,'head'=8] {'seq_0'}, dimensions={0}, use_global_device_ids=true | all-gather | bytes 320 | tf_op jit(solution)/shard_map/all_gather | solution.py:34
  89.2 1.0 copy.41
  90.2 1.3 copy.48
  91.9 3.8 %fusion.7 = f32[256,1,16,64]{0,3,2,1:T(8,128)} fusion(bf16[256,16,64]{0,2,1:T(8,128)(2,1)} %bitcast.184, f32[256,256]{1,0:T(8,128)S(1)} %fusion.63, f32[16,256]{1,0:T(8,128)S(1)} %compare_select_fusion.1, f32[16,256]{1,0:T(8,128)S(1)} %copy_bitcast_fusion, pred[256,256]{1,0:T(8,128)(4,1)S(1)} %iota_compare_fusion), kind=kOutput, calls=%fused_computation.8 | convolution fusion | flops 140509184 | bytes 1933312 | tf_op jit(solution)/shard_map/gjtu,ugjp->tgjp/dot_general | solution.py:314
  95.6 35.6 %all-gather.5.cloned.1.call-done = f32[4,1,16,64,256]{4,3,2,1,0:T(8,128)} async-done(((f32[1,1,16,64,256]{4,3,2,1,0:T(8,128)}), f32[4,1,16,64,256]{4,3,2,1,0:T(8,128)}) %all-gather.5.cloned.1.call-update) | async-done | bytes 4194320 | tf_op jit(solution)/shard_map/all_gather | solution.py:34
  131.3 6.0 %multiply_reduce_fusion = (f32[256]{0:T(256)S(1)}, f32[256,1,16,64]{0,3,2,1:T(8,128)}) fusion(f32[256,1,16,64]{0,3,2,1:T(8,128)S(1)} %bitcast.180, f32[256,1,16,64]{0,3,2,1:T(8,128)} %bitcast.181, f32[16]{0:T(128)S(1)} %bitcast.204, f32[256,1,16,64]{0,3,2,1:T(8,128)} %fusion.7, f32[256,16]{0,1:T(8,128)S(1)} %get-tuple-element.7, ...), kind=kOutput, calls=%fused_computation.37 | convolution fusion | flops 143130368 | bytes 12731976 | tf_op jit(solution)/shard_map/tgn,gjpn->tgjp/dot_general | solution.py:326
  137.3 1.6 copy.49
  139.3 88.3 %shard_map.127 = bf16[32,8192]{1,0:T(8,128)(2,1)S(1)} custom-call(bf16[256,1024]{1,0:T(8,128)(2,1)S(1)} %fusion.25.hid, bf16[1024,512]{1,0:T(8,128)(2,1)S(1)} %bitcast.177), custom_call_target="tpu_custom_call" | custom-call | tf_op jit(solution)/shard_map/pallas_call | solution.py:230
  227.6 0.8 copy.58
  (55 shorter events, 3.0 us)
Async XLA Ops:
  6.5 14.7 %copy-start.5 = (bf16[1,256,256]{2,1,0:T(8,128)(2,1)S(1)}, bf16[1,256,256]{2,1,0:T(8,128)(2,1)}, u32[]{:S(2)}) copy-start(bf16[1,256,256]{2,1,0:T(8,128)(2,1)} %param.14) | copy-start | bytes 393220
  6.5 69.9 %all-gather.7.cloned.1.call-start = ((), (), s32[]{:S(2)}) async-start(), calls=%async_computation.1 | async-start | bytes 5242880 | tf_op jit(solution)/shard_map/all_gather | solution.py:34
  8.0 10.2 %collective-permute-start = (bf16[3,1536]{1,0:T(4,128)(2,1)S(1)}, bf16[3,1536]{1,0:T(4,128)(2,1)S(1)}, u32[]{:S(2)}, u32[]{:S(2)}) collective-permute-start(bf16[3,1536]{1,0:T(4,128)(2,1)S(1)} %pad_maximum_fusion.3), channel_id=1, source_target_pairs={{0,8},{8,16},{16,24},{24,32},{32,40},{40,48},{48,56},{56,64},{64,7... | collective-permute-start | bytes 27656 | tf_op jit(solution)/shard_map/ppermute | solution.py:20
  21.4 58.7 %copy-start.2 = (bf16[1,256,1024]{2,1,0:T(8,128)(2,1)S(1)}, bf16[1,256,1024]{2,1,0:T(8,128)(2,1)}, u32[]{:S(2)}) copy-start(bf16[1,256,1024]{2,1,0:T(8,128)(2,1)} %param.16) | copy-start | bytes 1572868
  22.7 66.2 %copy-start.9 = (f32[1,4,256]{2,1,0:T(4,128)S(1)}, f32[1,4,256]{2,1,0:T(4,128)}, u32[]{:S(2)}) copy-start(f32[1,4,256]{2,1,0:T(4,128)} %param.20) | copy-start | bytes 12292
  22.7 66.2 %copy-start.4 = (f32[1,16,256]{2,1,0:T(8,128)S(1)}, f32[1,16,256]{2,1,0:T(8,128)}, u32[]{:S(2)}) copy-start(f32[1,16,256]{2,1,0:T(8,128)} %param.17) | copy-start | bytes 49156
  22.7 66.2 %copy-start.7 = (f32[1,16]{1,0:T(1,128)S(1)}, f32[1,16]{1,0:T(1,128)}, u32[]{:S(2)}) copy-start(f32[1,16]{1,0:T(1,128)} %param.22) | copy-start | bytes 196
  22.7 108.5 %all-gather.5.cloned.1.call-start = ((), (), s32[]{:S(2)}) async-start(), calls=%async_computation | async-start | bytes 5242880 | tf_op jit(solution)/shard_map/all_gather | solution.py:34
  76.4 15.0 %copy-start.6 = (bf16[1,256,256]{2,1,0:T(8,128)(2,1)S(1)}, bf16[1,256,256]{2,1,0:T(8,128)(2,1)}, u32[]{:S(2)}) copy-start(bf16[1,256,256]{2,1,0:T(8,128)(2,1)} %param.15) | copy-start | bytes 393220
  91.6 39.7 %copy-start.1 = (f32[1,1,16,64,256]{4,3,2,1,0:T(8,128)S(1)}, f32[1,1,16,64,256]{4,3,2,1,0:T(8,128)}, u32[]{:S(2)}) copy-start(f32[1,1,16,64,256]{4,3,2,1,0:T(8,128)} %fusion.15) | copy-start | bytes 3145732
  91.6 39.7 %copy-start.10 = (f32[1,16]{1,0:T(1,128)S(1)}, f32[1,16]{1,0:T(1,128)}, u32[]{:S(2)}) copy-start(f32[1,16]{1,0:T(1,128)} %param.23) | copy-start | bytes 196
  91.8 39.5 %copy-start.3 = (f32[1,256,1024]{1,2,0:T(8,128)S(1)}, f32[1,256,1024]{1,2,0:T(8,128)}, u32[]{:S(2)}) copy-start(f32[1,256,1024]{1,2,0:T(8,128)} %copy.50) | copy-start | bytes 3145732
  131.3 7.6 %copy-start.8 = (f32[1,1024]{1,0:T(1,128)S(1)}, f32[1,1024]{1,0:T(1,128)}, u32[]{:S(2)}) copy-start(f32[1,1024]{1,0:T(1,128)} %param.24) | copy-start | bytes 12292
  137.3 2.1 copy-start
Sparse Core Ops, SparseCore 0:
  22.8 53.5 all-gather.6
  80.2 51.0 all-gather.4

commit v2 on v0

v2 whole, which is shorter than its diff:
```python
import jax
import jax.numpy as jnp
from jax import lax
from jax.experimental import pallas as pl
from jax.experimental.pallas import tpu as pltpu
from jax.sharding import Mesh
from jax.sharding import PartitionSpec as P

SEQ = ("seq_0", "seq_1")
SEQ_HEAD = ("seq_0", "seq_1", "head")
MESH = pl.DeviceIdType.MESH
PIECES = (4, 3, 5, 2, 6, 1, 7, 0)
OFFSETS = (0, 3, 1, 2)
PEERS = tuple((dx, dy) for dx in (2, 1, 3, 0) for dy in (2, 1, 3, 0) if dx or dy)
W_CUTS = (0, 256, 512, 1024)
F32 = jnp.float32
BF16 = jnp.bfloat16

epsilon = 1e-05


def send(src, dst, send_sem, recv_sem, **to):
    return pltpu.make_async_remote_copy(
        src_ref=src, dst_ref=dst, send_sem=send_sem, recv_sem=recv_sem,
        device_id=to, device_id_type=MESH,
    )


def exact_dot(a, b):
    return jnp.dot(a, b, precision=lax.Precision.HIGHEST, preferred_element_type=F32)


def conv_blocks(padded, kernel, out, blocks):
    def columns(i, _):
        cols = pl.ds(pl.multiple_of(i * 256, 256), 256)
        for block in blocks:
            summed = jnp.zeros((64, 256), F32)
            for k in range(4):
                summed = summed + kernel[k : k + 1, cols] * padded[block * 64 + 5 + k : block * 64 + 69 + k, cols]
            out[block * 64 : block * 64 + 64, cols] = (summed * jax.nn.sigmoid(summed)).astype(BF16)
        return 0

    lax.fori_loop(0, out.shape[1] // 256, columns, 0)


def mixer_kernel(
    x_in, b_in, c_in, z_in, dt, conv_x, conv_b, conv_c, rate, bias, skip, gain, w, out,
    halo_x, halo_b, halo_c, pad_x, pad_b, pad_c, xc, bc, cc, xw,
    step, logd, decay_own, decay, state, state_in, state_out, carried, scores, inside, grow, to_end,
    wg, ag, ring_out, ring_in, done,
    h_send, h_recv, d_send, d_recv, s_send, s_recv, t_send, t_recv,
    w_own, w_send, w_recv, wf_send, wf_recv, a_send, a_recv, r_send, r_recv, o_send, o_recv,
):
    s, x, y, h = (lax.axis_index(a) for a in ("section", "seq_0", "seq_1", "head"))
    q = x * 4 + y
    xr, xl = lax.rem(x + 1, 4), lax.rem(x + 3, 4)
    ys = [lax.rem(y + o, 4) for o in OFFSETS]
    sides = (lax.rem(h + 1, 8), lax.rem(h + 7, 8))
    peers = [(lax.rem(x + dx, 4), lax.rem(y + dy, 4)) for dx, dy in PEERS]

    barrier = pltpu.get_barrier_semaphore()
    greeted = (
        [{"seq_0": u, "seq_1": v} for u, v in peers]
        + [{"head": v} for v in sides]
        + [{"section": 1 - s, "seq_1": v} for v in ys]
    )
    for peer in greeted:
        pl.semaphore_signal(barrier, inc=1, device_id=peer, device_id_type=MESH)

    own_w = pltpu.make_async_copy(w, wg.at[0], w_own)
    own_w.start()

    started = []

    def start(copies):
        for c in copies:
            c.start()
        started.extend(copies)
        return copies

    row16 = lax.broadcasted_iota(jnp.int32, (16, 16), 0)
    col16 = lax.broadcasted_iota(jnp.int32, (16, 16), 1)

    def column(row):
        return jnp.sum(jnp.where(row16 == col16, jnp.broadcast_to(row, (16, 16)), 0.0), axis=1, keepdims=True)

    raw = dt[...] + column(bias[...])
    step_size = jnp.maximum(raw, 0.0) + jnp.log1p(jnp.exp(-jnp.abs(raw)))
    log_decay = -column(rate[...]) * step_size
    lane = lax.broadcasted_iota(jnp.int32, (16, 256), 1)
    for shift in (1, 2, 4, 8, 16, 32, 64, 128):
        log_decay = log_decay + jnp.where(lane >= shift, pltpu.roll(log_decay, shift, 1), 0.0)
    step[...] = step_size
    logd[...] = log_decay
    spread = jnp.where(
        lax.shift_right_logical(lax.broadcasted_iota(jnp.int32, (16, 1024), 1), 6)
        == lax.broadcasted_iota(jnp.int32, (16, 1024), 0), 1.0, 0.0,
    ).astype(F32)
    log_cols = log_decay.T
    end_cols = (jnp.exp(log_decay[:, 255:256] - log_decay) * step_size).T
    last = exact_dot(jnp.exp(log_cols[248:256, :]), spread)[7:8, :]
    for r in range(8):
        decay_own[r : r + 1, :] = last[:, r * 128 : r * 128 + 128]
    decay[q] = decay_own[...]

    pl.semaphore_wait(barrier, len(greeted))

    to_next = {"seq_0": lax.rem(x + lax.div(y + 1, 4), 4), "seq_1": lax.rem(y + 1, 4)}
    halo = start([
        send(src.at[pl.ds(240, 16)], dst, h_send.at[i], h_recv.at[i], **to_next)
        for i, (src, dst) in enumerate(((b_in, halo_b), (x_in, halo_x), (c_in, halo_c)))
    ])
    decays = start([
        send(decay_own, decay.at[q], d_send.at[i], d_recv.at[i], seq_0=u, seq_1=v)
        for i, (u, v) in enumerate(peers)
    ])

    def w_part(i):
        n = W_CUTS[i + 1] - W_CUTS[i]
        plus, minus = pl.ds(W_CUTS[i], n), pl.ds(1024 - W_CUTS[i + 1], n)
        return [
            send(w.at[plus], wg.at[1, plus], w_send.at[0, i], w_recv.at[0, i], seq_0=xr),
            send(w.at[minus], wg.at[2, minus], w_send.at[1, i], w_recv.at[1, i], seq_0=xl),
        ]

    w_direct = [start(w_part(0))]

    pad_x[8:264, :] = x_in[...].astype(F32)
    pad_b[8:264, :] = b_in[...].astype(F32)
    pad_c[8:264, :] = c_in[...].astype(F32)
    to_end[...] = exact_dot(end_cols, spread)
    conv_blocks(pad_b, conv_b, bc, (1, 2, 3))
    conv_blocks(pad_x, conv_x, xc, (1, 2, 3))

    def finish(i, halo_ref, padded, kernel, conv_out):
        halo[i].wait_recv()
        padded[0:8, :] = jnp.where(q > 0, halo_ref[...].astype(F32)[8:16], 0.0)
        conv_blocks(padded, kernel, conv_out, (0,))

    finish(0, halo_b, pad_b, conv_b, bc)
    finish(1, halo_x, pad_x, conv_x, xc)

    b_cols = bc[...].astype(F32).T.astype(BF16)
    for i in range(4):
        cols = slice(i * 256, i * 256 + 256)
        xw[:, cols] = (xc[:, cols].astype(F32) * to_end[:, cols]).astype(BF16)
        state[:, cols] = jnp.dot(b_cols, xw[:, cols], preferred_element_type=F32).astype(BF16)
    state_in[q] = state[pl.ds(pl.multiple_of(q * 16, 16), 16), :]
    sums = start([
        send(
            state.at[pl.ds(pl.multiple_of((u * 4 + v) * 16, 16), 16)], state_in.at[q],
            s_send.at[i], s_recv.at[i], seq_0=u, seq_1=v,
        )
        for i, (u, v) in enumerate(peers)
    ])
    w_direct.append(start(w_part(1)))

    conv_blocks(pad_c, conv_c, cc, (1, 2, 3))
    finish(2, halo_c, pad_c, conv_c, cc)
    scores[...] = lax.dot_general(cc[...], bc[...], (((1,), (1,)), ((), ())), preferred_element_type=F32)
    skip_row = exact_dot(jnp.broadcast_to(skip[...], (8, 16)), spread)[0:1, :]
    causal = lax.broadcasted_iota(jnp.int32, (128, 128), 0) >= lax.broadcasted_iota(jnp.int32, (128, 128), 1)
    first_half = lax.broadcasted_iota(jnp.int32, (256, 128), 1) < 64
    grow_cols = jnp.exp(log_cols)

    def damped(log_col, head, rows, cols, masked):
        value = jnp.exp(jnp.minimum(log_col[rows] - logd[head : head + 1, cols], 0.0))
        if masked:
            value = jnp.where(causal, value, 0.0)
        return (value * step[head : head + 1, cols] * scores[rows, cols]).astype(BF16)

    top, bottom = slice(0, 128), slice(128, 256)

    def pair(g):
        lanes = slice(g * 128, g * 128 + 128)
        parts = []
        for head in (2 * g, 2 * g + 1):
            log_col = log_cols[:, head : head + 1]
            upper = jnp.dot(damped(log_col, head, top, top, True), xc[top, lanes], preferred_element_type=F32)
            lower = jnp.dot(damped(log_col, head, bottom, top, False), xc[top, lanes], preferred_element_type=F32)
            lower = lower + jnp.dot(damped(log_col, head, bottom, bottom, True), xc[bottom, lanes], preferred_element_type=F32)
            parts.append(jnp.concatenate([upper, lower], axis=0))
        both = jnp.where(first_half, parts[0], parts[1])
        zf = z_in[:, lanes].astype(F32)
        gate = zf * jax.nn.sigmoid(zf)
        inside[:, lanes] = (both + skip_row[:, lanes] * xc[:, lanes].astype(F32)) * gate
        grow[:, lanes] = exact_dot(grow_cols, spread[:, lanes]) * gate

    for g in range(4):
        pair(g)

    for c in decays + sums:
        c.wait_recv()
    for r in range(8):
        lanes = slice(r * 128, r * 128 + 128)
        acc = jnp.zeros((16, 128), F32)
        for k in range(16):
            state_out[k, :, lanes] = acc.astype(BF16)
            if k < 15:
                acc = decay[k, r : r + 1, :] * acc + state_in[k, :, lanes].astype(F32)
    my_rows = pl.ds(pl.multiple_of(q * 16, 16), 16)
    entering = start([
        send(state_out.at[u * 4 + v], carried.at[my_rows], t_send.at[i], t_recv.at[i], seq_0=u, seq_1=v)
        for i, (u, v) in enumerate(peers)
    ])
    carried[my_rows, :] = state_out[q]
    w_direct.append(start(w_part(2)))

    for g in range(4, 8):
        pair(g)
    for side in (0, 1):
        for j in range(4):
            ring_in[side, 0, j, :, 256 - 256 * side : 512 - 256 * side] = jnp.zeros((128, 256), BF16)

    def w_forward(i):
        n = W_CUTS[i + 1] - W_CUTS[i]
        plus, minus = pl.ds(W_CUTS[i], n), pl.ds(1024 - W_CUTS[i + 1], n)
        return [
            send(wg.at[1, plus], wg.at[3, plus], wf_send.at[0, i], wf_recv.at[0, i], seq_0=xr),
            send(wg.at[2, minus], wg.at[3, minus], wf_send.at[1, i], wf_recv.at[1, i], seq_0=xl),
        ]

    w_passed = []

    def forward_w(i):
        for c in w_direct[i]:
            c.wait_recv()
        w_passed.extend(start(w_forward(i)))

    def a_direct(p):
        mine = ag.at[pl.ds(p * 128, 32)]
        copies = [
            send(mine, ag.at[pl.ds(p * 128 + 32, 32)], a_send.at[p, 0], a_recv.at[p, 0], seq_1=ys[2]),
            send(mine, ag.at[pl.ds(p * 128 + 64, 32)], a_send.at[p, 1], a_recv.at[p, 1], seq_1=ys[1]),
        ]
        if p == 0:
            copies.append(send(mine, ag.at[pl.ds(96, 32)], a_send.at[p, 2], a_recv.at[p, 2], seq_1=ys[3]))
        return copies

    def a_forward(p):
        return [
            send(ag.at[pl.ds(p * 128 + 32, 16)], ag.at[pl.ds(p * 128 + 96, 16)], a_send.at[p, 2], a_recv.at[p, 2], seq_1=ys[2]),
            send(ag.at[pl.ds(p * 128 + 80, 16)], ag.at[pl.ds(p * 128 + 112, 16)], a_send.at[p, 3], a_recv.at[p, 3], seq_1=ys[1]),
        ]

    direct = {p: a_direct(p) for p in range(8)}
    passed = {p: a_forward(p) for p in range(1, 8)}

    for c in entering:
        c.wait_recv()

    def hidden(p):
        rows = pl.ds(pl.multiple_of(lax.rem(h + PIECES[p], 8) * 32, 32), 32)
        outside = jnp.dot(cc[rows, :], carried[...], preferred_element_type=F32)
        gated = inside[rows, :] + outside * grow[rows, :]
        inverse_rms = lax.rsqrt(jnp.mean(gated * gated, axis=1, keepdims=True) + epsilon)
        ag[p * 128 : p * 128 + 32, :] = (gated * inverse_rms * gain[...]).astype(BF16)

    hidden(0)
    hidden(1)
    start(direct[0])
    hidden(2)
    start(direct[1])
    hidden(3)
    start(direct[2])
    for p in range(4, 8):
        hidden(p)
    own_w.wait()
    forward_w(0)

    def forward(p):
        direct[p][0].wait_recv()
        start(passed[p][:1])
        direct[p][1].wait_recv()
        start(passed[p][1:])

    def arrived(p):
        for c in passed[p]:
            c.wait_recv()

    def ring(stage, j, side):
        axis = {"head": sides[side]}
        src, dst = ring_out.at[side, stage, j], ring_in.at[side, stage, j]
        if stage == 0:
            half = pl.ds(side * 256, 256)
            src, dst = src.at[:, half], dst.at[:, half]
        return send(src, dst, r_send.at[side, stage, j], r_recv.at[side, stage, j], **axis)

    rings = {(stage, j): [ring(stage, j, side) for side in (0, 1)] for stage in range(4) for j in range(4)}

    def first(j):
        part = jnp.dot(ag[0:128, :], wg[j], preferred_element_type=F32)
        ring_out[0, 0, j, :, :256] = part[:, :256].astype(BF16)
        ring_out[1, 0, j, :, 256:] = part[:, 256:].astype(BF16)
        start(rings[0, j])

    def middle(stage, j):
        p = 2 * stage - 1
        part = jnp.dot(ag[p * 128 : p * 128 + 256, :], wg[j], preferred_element_type=F32)
        for side in (0, 1):
            rings[stage - 1, j][side].wait_recv()
            got = ring_in[side, stage - 1, j].astype(F32)
            ring_out[side, stage, j] = (part[side * 128 : side * 128 + 128] + got).astype(BF16)
        start(rings[stage, j])

    results = []

    def final(j):
        part = jnp.dot(ag[896:1024, :], wg[j], preferred_element_type=F32)
        for side in (0, 1):
            rings[3, j][side].wait_recv()
        total = part + ring_in[0, 3, j].astype(F32) + ring_in[1, 3, j].astype(F32)
        done[j] = total.astype(BF16)
        cols = pl.ds(pl.multiple_of((lax.rem(x + OFFSETS[j], 4) * 4 + y) * 512, 512), 512)
        copies = [
            send(done.at[j, pl.ds(r * 32, 32)], out.at[:, cols], o_send.at[r, j], o_recv.at[r, j], section=1 - s, seq_1=ys[r])
            for r in range(4)
        ]
        results.extend(start(copies))

    for c in direct[0]:
        c.wait_recv()
    first(0)
    forward_w(1)
    for c in w_direct[2]:
        c.wait_recv()
    first(1)
    first(2)
    forward(1)
    forward(2)
    start(direct[3])
    start(direct[4])
    arrived(1)
    arrived(2)
    for j in range(3):
        middle(1, j)
    forward(3)
    forward(4)
    start(direct[5])
    start(direct[6])
    for c in w_passed:
        c.wait_recv()
    first(3)
    arrived(3)
    arrived(4)
    for j in range(3):
        middle(2, j)
    forward(5)
    forward(6)
    start(direct[7])
    middle(1, 3)
    arrived(5)
    arrived(6)
    for j in range(3):
        middle(3, j)
    forward(7)
    middle(2, 3)
    middle(3, 3)
    arrived(7)
    for j in range(4):
        final(j)

    for c in started:
        c.wait_send()
    for c in results:
        c.wait_recv()


def per_device(
    x_in, b_in, c_in, z_in, dt_raw, conv_x, conv_b, conv_c, a_rate, dt_bias, skip_d, norm_gain, out_weight
):
    dma = pltpu.SemaphoreType.DMA
    half = lambda *shape: pltpu.VMEM(shape, BF16)
    full = lambda *shape: pltpu.VMEM(shape, F32)
    in_vmem = pl.BlockSpec(memory_space=pltpu.VMEM)
    anywhere = pl.BlockSpec(memory_space=pl.ANY)
    mixed = pl.pallas_call(
        mixer_kernel,
        out_shape=jax.ShapeDtypeStruct((32, 8192), BF16),
        in_specs=[in_vmem] * 12 + [anywhere],
        out_specs=anywhere,
        scratch_shapes=[
            half(16, 1024), half(16, 256), half(16, 256), full(264, 1024), full(264, 256), full(264, 256),
            half(256, 1024), half(256, 256), half(256, 256), half(256, 1024),
            full(16, 256), full(16, 256), full(8, 128), full(16, 8, 128),
            half(256, 1024), half(16, 16, 1024), half(16, 16, 1024), half(256, 1024),
            full(256, 256), full(256, 1024), full(256, 1024), full(256, 1024),
            half(4, 1024, 512), half(1024, 1024), half(2, 4, 4, 128, 512), half(2, 4, 4, 128, 512), half(4, 128, 512),
            dma((3,)), dma((3,)), dma((15,)), dma((15,)), dma((15,)), dma((15,)), dma((15,)), dma((15,)),
            dma, dma((2, 3)), dma((2, 3)), dma((2, 2)), dma((2, 2)), dma((8, 4)), dma((8, 4)),
            dma((2, 4, 4)), dma((2, 4, 4)), dma((4, 4)), dma((4, 4)),
        ],
        compiler_params=pltpu.CompilerParams(
            collective_id=0, has_side_effects=True, vmem_limit_bytes=56 * 2**20
        ),
    )(
        x_in[0], b_in[0], c_in[0], z_in[0], dt_raw[0], conv_x[0], conv_b[0], conv_c[0],
        a_rate, dt_bias, skip_d, norm_gain, out_weight[0],
    )
    return mixed[None]


def solution(mesh):
    finer = Mesh(
        mesh.devices.reshape(mesh.shape["section"], 4, 4, mesh.shape["head"]),
        ("section", "seq_0", "seq_1", "head"),
    )
    return jax.shard_map(
        per_device,
        mesh=finer,
        in_specs=(
            P("section", SEQ, "head"),
            P("section", SEQ, "head"),
            P("section", SEQ, "head"),
            P("section", SEQ, "head"),
            P("section", "head", SEQ),
            P("section", None, "head"),
            P("section", None, "head"),
            P("section", None, "head"),
            P("section", "head"),
            P("section", "head"),
            P("section", "head"),
            P("section", "head"),
            P("section", "head", SEQ),
        ),
        out_specs=P("section", SEQ_HEAD, None),
        check_vma=False,
    )
```

time: 361 us -> 99.9 us (0.28)
  waiting for transfers between devices: 219 us -> 0 us
  Pallas kernels: 0 us -> 97.9 us
  blocking collectives: 66.2 us -> 0 us
  matrix products: 19.9 us -> 0 us
  starting transfers between devices: 15 us -> 0 us
  between operations: 13.4 us -> 0.01 us
  local copies, waits for them, and re-layouts: 14.5 us -> 1.87 us
  other arithmetic: 12.5 us -> 0 us
    all_gather x3 -> x0, waiting for transfers between devices: 142 us -> none  [the longest x2 84.7 us: entering(): pieces = jax.tree.map(lambda part: lax.all_gather(part, axis), so_far)]
    pallas_call x0 -> x1, Pallas kernels: none -> 97.9 us  [per_device(): pl.pallas_call(mixer_kernel, out_shape=jax.ShapeDtypeStruct((32, 8192), B...]
    all_to_all x1 -> x0, waiting for transfers between devices: 74.1 us -> none  [from_everyone(): lax.all_to_all(jnp.broadcast_to(x[None], (size, *x.shape)), axis, 0, 0, t...]
    all_to_all x2 -> x0, blocking collectives: 49.6 us -> none  [the longest x1 29.7 us: per_device(): lax.all_to_all(hidden, 'head', split_axis=0, concat_axis=1, tiled=True)]
    dot_general x5 -> x0, matrix products: 19.9 us -> none  [the longest x1 10.2 us: per_device(): jnp.dot(collect(owned_rows, SEQ, 0), full_columns, preferred_element_type...]
    all_gather x2 -> x0, blocking collectives: 16.6 us -> none  [entering(): pieces = jax.tree.map(lambda part: lax.all_gather(part, axis), so_far)]
    ppermute x2 -> x0, starting transfers between devices: 9.23 us -> none  [the longest x1 5.19 us: passed_along_2(): return lax.ppermute(block, axis, route)]
    convert_element_type x5 -> x0, other arithmetic: 5.74 us -> none  [the longest x1 1.59 us: per_device(): ((gated * inverse_rms).reshape(length, x_cols) * norm_gain[0]).astype(jnp...]
  transfers between devices with their start and end apart: 6 -> 0, of which waited for: 6 -> 0; matrix products, arithmetic and copies ran while one was open for 7% -> 0% of each run, Pallas kernels for 0% -> 0%
where the time goes in v2:
time: 99.9 us; the launch traced here: 99.8 us
  Pallas kernels  97.9 us (98%)
  local copies, waits for them, and re-layouts  1.87 us (2%)
    pallas_call x1, Pallas kernels, per_device(): pl.pallas_call(mixer_kernel, out_shape=jax.ShapeDtypeStruct((32, 8192), B...  97.9 us

profile of v2, /device:TPU:1, one launch (start us, length us, event | category | flops | bytes accessed | tf_op | source)
XLA Modules:
  0.0 99.8 jit_solution(602339905143166083)
XLA Ops:
  0.0 97.9 %shard_map.127 = bf16[32,8192]{1,0:T(8,128)(2,1)} custom-call(bf16[256,1024]{1,0:T(8,128)(2,1)} %bitcast.12, bf16[256,256]{1,0:T(8,128)(2,1)} %bitcast.14, bf16[256,256]{1,0:T(8,128)(2,1)} %bitcast.15, bf16[256,1024]{1,0:T(8,128)(2,1)} %bitcast.13, f32[16,256]{1,0:T(8,128)} %bitcast.16, f32[4,1024]{1,0:T(4,128)} %bitcast.17, f32[4,256]{1,0:T(4,128)} %bitcast.18, ...), custom_call_target="tpu_custom_call" | custom-call | tf_op jit(solution)/shard_map/pallas_call | solution.py:377
  97.9 1.9 %copy.15 = bf16[1,32,8192]{2,1,0:T(8,128)(2,1)} copy(bf16[1,32,8192]{2,1,0:T(8,128)(2,1)} %bitcast.10) | data formatting | bytes 1048576

commit v3 on v2

v3 whole, which is shorter than its diff:
```python
import jax
import jax.numpy as jnp
from jax import lax
from jax.experimental import pallas as pl
from jax.experimental.pallas import tpu as pltpu
from jax.sharding import Mesh
from jax.sharding import PartitionSpec as P

SEQ = ("seq_0", "seq_1")
SEQ_HEAD = ("seq_0", "seq_1", "head")
MESH = pl.DeviceIdType.MESH
PIECES = (4, 3, 5, 2, 6, 1, 7, 0)
OFFSETS = (0, 3, 1, 2)
PEERS = tuple((dx, dy) for dx in (2, 1, 3, 0) for dy in (2, 1, 3, 0) if dx or dy)
W_CUTS = (0, 336, 672, 1024)
ROWS = ((0, 32), (32, 64), (96, 32), (0, 128))
F32 = jnp.float32
BF16 = jnp.bfloat16

epsilon = 1e-05


def send(src, dst, send_sem, recv_sem, **to):
    return pltpu.make_async_remote_copy(
        src_ref=src, dst_ref=dst, send_sem=send_sem, recv_sem=recv_sem,
        device_id=to, device_id_type=MESH,
    )


def exact_dot(a, b):
    return jnp.dot(a, b, precision=lax.Precision.HIGHEST, preferred_element_type=F32)


def conv_blocks(padded, kernel, out, blocks):
    def columns(i, _):
        cols = pl.ds(pl.multiple_of(i * 256, 256), 256)
        for block in blocks:
            summed = jnp.zeros((64, 256), F32)
            for k in range(4):
                summed = summed + kernel[k : k + 1, cols] * padded[block * 64 + 5 + k : block * 64 + 69 + k, cols]
            out[block * 64 : block * 64 + 64, cols] = (summed * jax.nn.sigmoid(summed)).astype(BF16)
        return 0

    lax.fori_loop(0, out.shape[1] // 256, columns, 0)


def mixer_kernel(
    x_hbm, b_hbm, c_hbm, z_hbm, dt_hbm, conv_x_hbm, conv_b_hbm, conv_c_hbm, rate_hbm, bias_hbm, skip_hbm, gain_hbm, w, out,
    x_in, b_in, c_in, z_in, dt, conv_x, conv_b, conv_c, rate, bias, skip, gain,
    halo_x, halo_b, halo_c, pad_x, pad_b, pad_c, xc, bc, cc, xw,
    step, logd, decay_own, decay, state, state_in, state_out, carried, scores, inside, grow, to_end,
    wg, ag, ring_out, ring_in, done,
    l_sem, h_send, h_recv, d_sem, s_sem, t_sem,
    w_own, w_send, w_recv, wf_send, wf_recv, f_send, f_recv, a_send, a_recv, r_send, r_recv, o_sem,
):
    s, x, y, h = (lax.axis_index(a) for a in ("section", "seq_0", "seq_1", "head"))
    q = x * 4 + y
    ring_at = [[lax.rem(v + o, 4) for o in OFFSETS] for v in (x, y)]
    sides = (lax.rem(h + 1, 8), lax.rem(h + 7, 8))
    peers = [(lax.rem(x + dx, 4), lax.rem(y + dy, 4)) for dx, dy in PEERS]

    barrier = pltpu.get_barrier_semaphore()
    greeted = (
        [{"seq_0": u, "seq_1": v} for u, v in peers]
        + [{"head": v} for v in sides]
        + [{"section": 1 - s, "seq_1": v} for v in ring_at[1]]
        + [{"section": 1 - s, "seq_0": v} for v in ring_at[0][1:]]
    )
    for peer in greeted:
        pl.semaphore_signal(barrier, inc=1, device_id=peer, device_id_type=MESH)

    loads = {}
    for i, (name, src, dst) in enumerate((
        ("dt", dt_hbm, dt), ("bias", bias_hbm, bias), ("rate", rate_hbm, rate),
        ("b", b_hbm, b_in), ("x", x_hbm, x_in), ("c", c_hbm, c_in),
        ("kb", conv_b_hbm, conv_b), ("kx", conv_x_hbm, conv_x), ("kc", conv_c_hbm, conv_c),
        ("skip", skip_hbm, skip), ("z", z_hbm, z_in), ("gain", gain_hbm, gain),
    )):
        loads[name] = pltpu.make_async_copy(src, dst, l_sem.at[i])
        loads[name].start()
    own_w = [pltpu.make_async_copy(w.at[:, pl.ds(a * 256, 256)], wg.at[a, 0], w_own.at[a]) for a in (0, 1)]
    for c in own_w:
        c.start()

    def loaded(*names):
        for n in names:
            loads[n].wait()

    def all_of(ref, sem):
        pltpu.make_async_copy(ref, ref, sem).wait()

    def start(copies):
        for c in copies:
            c.start()

    loaded("dt", "bias", "rate")
    row16 = lax.broadcasted_iota(jnp.int32, (16, 16), 0)
    col16 = lax.broadcasted_iota(jnp.int32, (16, 16), 1)

    def column(row):
        return jnp.sum(jnp.where(row16 == col16, jnp.broadcast_to(row, (16, 16)), 0.0), axis=1, keepdims=True)

    raw = dt[...] + column(bias[...])
    step_size = jnp.maximum(raw, 0.0) + jnp.log1p(jnp.exp(-jnp.abs(raw)))
    log_decay = -column(rate[...]) * step_size
    lane = lax.broadcasted_iota(jnp.int32, (16, 256), 1)
    for shift in (1, 2, 4, 8, 16, 32, 64, 128):
        log_decay = log_decay + jnp.where(lane >= shift, pltpu.roll(log_decay, shift, 1), 0.0)
    step[...] = step_size
    logd[...] = log_decay
    spread = jnp.where(
        lax.shift_right_logical(lax.broadcasted_iota(jnp.int32, (16, 1024), 1), 6)
        == lax.broadcasted_iota(jnp.int32, (16, 1024), 0), 1.0, 0.0,
    ).astype(F32)
    log_cols = log_decay.T
    end_cols = (jnp.exp(log_decay[:, 255:256] - log_decay) * step_size).T
    last = exact_dot(jnp.exp(log_cols[248:256, :]), spread)[7:8, :]
    for r in range(8):
        decay_own[r : r + 1, :] = last[:, r * 128 : r * 128 + 128]
    decay[q] = decay_own[...]

    loaded("b", "x", "c")
    pl.semaphore_wait(barrier, len(greeted))

    to_next = {"seq_0": lax.rem(x + lax.div(y + 1, 4), 4), "seq_1": lax.rem(y + 1, 4)}
    halo = [
        send(src.at[pl.ds(240, 16)], dst, h_send.at[i], h_recv.at[i], **to_next)
        for i, (src, dst) in enumerate(((b_in, halo_b), (x_in, halo_x), (c_in, halo_c)))
    ]

    @pl.when(q < 15)
    def _():
        for c in halo:
            c.start()

    start([
        send(decay_own, decay.at[q], d_sem.at[0], d_sem.at[1], seq_0=u, seq_1=v)
        for i, (u, v) in enumerate(peers)
    ])

    def w_part(i):
        n = W_CUTS[i + 1] - W_CUTS[i]
        plus, minus = pl.ds(W_CUTS[i], n), pl.ds(1024 - W_CUTS[i + 1], n)
        copies = []
        for a in (0, 1):
            cols = pl.ds(a * 256, 256)
            copies += [
                send(w.at[plus, cols], wg.at[a, 1, plus], w_send, w_recv.at[a, 0], **{SEQ[a]: ring_at[a][2]}),
                send(w.at[minus, cols], wg.at[a, 2, minus], w_send, w_recv.at[a, 1], **{SEQ[a]: ring_at[a][1]}),
            ]
        return copies

    start(w_part(0))

    loaded("kb", "kx", "kc", "skip", "z", "gain")
    pad_x[8:264, :] = x_in[...].astype(F32)
    pad_b[8:264, :] = b_in[...].astype(F32)
    pad_c[8:264, :] = c_in[...].astype(F32)
    to_end[...] = exact_dot(end_cols, spread)
    conv_blocks(pad_b, conv_b, bc, (1, 2, 3))
    conv_blocks(pad_x, conv_x, xc, (1, 2, 3))

    def finish(i, halo_ref, padded, kernel, conv_out):
        @pl.when(q > 0)
        def _():
            halo[i].wait_recv()
            padded[0:8, :] = halo_ref[...].astype(F32)[8:16]

        @pl.when(q == 0)
        def _():
            padded[0:8, :] = jnp.zeros((8, padded.shape[1]), F32)

        conv_blocks(padded, kernel, conv_out, (0,))

    finish(0, halo_b, pad_b, conv_b, bc)
    finish(1, halo_x, pad_x, conv_x, xc)

    b_cols = bc[...].astype(F32).T.astype(BF16)
    for i in range(4):
        cols = slice(i * 256, i * 256 + 256)
        xw[:, cols] = (xc[:, cols].astype(F32) * to_end[:, cols]).astype(BF16)
        state[:, cols] = jnp.dot(b_cols, xw[:, cols], preferred_element_type=F32).astype(BF16)
    state_in[q] = state[pl.ds(pl.multiple_of(q * 16, 16), 16), :]
    start([
        send(
            state.at[pl.ds(pl.multiple_of((u * 4 + v) * 16, 16), 16)], state_in.at[q],
            s_sem.at[0], s_sem.at[1], seq_0=u, seq_1=v,
        )
        for i, (u, v) in enumerate(peers)
    ])
    start(w_part(1))

    conv_blocks(pad_c, conv_c, cc, (1, 2, 3))
    finish(2, halo_c, pad_c, conv_c, cc)
    scores[...] = lax.dot_general(cc[...], bc[...], (((1,), (1,)), ((), ())), preferred_element_type=F32)
    skip_row = exact_dot(jnp.broadcast_to(skip[...], (8, 16)), spread)[0:1, :]
    causal = lax.broadcasted_iota(jnp.int32, (128, 128), 0) >= lax.broadcasted_iota(jnp.int32, (128, 128), 1)
    first_half = lax.broadcasted_iota(jnp.int32, (256, 128), 1) < 64
    grow_cols = jnp.exp(log_cols)

    def damped(log_col, head, rows, cols, masked):
        value = jnp.exp(jnp.minimum(log_col[rows] - logd[head : head + 1, cols], 0.0))
        if masked:
            value = jnp.where(causal, value, 0.0)
        return (value * step[head : head + 1, cols] * scores[rows, cols]).astype(BF16)

    top, bottom = slice(0, 128), slice(128, 256)

    def pair(g):
        lanes = slice(g * 128, g * 128 + 128)
        parts = []
        for head in (2 * g, 2 * g + 1):
            log_col = log_cols[:, head : head + 1]
            upper = jnp.dot(damped(log_col, head, top, top, True), xc[top, lanes], preferred_element_type=F32)
            lower = jnp.dot(damped(log_col, head, bottom, top, False), xc[top, lanes], preferred_element_type=F32)
            lower = lower + jnp.dot(damped(log_col, head, bottom, bottom, True), xc[bottom, lanes], preferred_element_type=F32)
            parts.append(jnp.concatenate([upper, lower], axis=0))
        both = jnp.where(first_half, parts[0], parts[1])
        zf = z_in[:, lanes].astype(F32)
        gate = zf * jax.nn.sigmoid(zf)
        inside[:, lanes] = (both + skip_row[:, lanes] * xc[:, lanes].astype(F32)) * gate
        grow[:, lanes] = exact_dot(grow_cols, spread[:, lanes]) * gate

    for g in range(4):
        pair(g)

    all_of(decay.at[pl.ds(0, 15)], d_sem.at[1])
    all_of(state.at[pl.ds(0, 240)], s_sem.at[1])
    for r in range(8):
        lanes = slice(r * 128, r * 128 + 128)
        acc = jnp.zeros((16, 128), F32)
        for k in range(16):
            state_out[k, :, lanes] = acc.astype(BF16)
            if k < 15:
                acc = decay[k, r : r + 1, :] * acc + state_in[k, :, lanes].astype(F32)
    my_rows = pl.ds(pl.multiple_of(q * 16, 16), 16)
    start([
        send(state_out.at[u * 4 + v], carried.at[my_rows], t_sem.at[0], t_sem.at[1], seq_0=u, seq_1=v)
        for i, (u, v) in enumerate(peers)
    ])
    carried[my_rows, :] = state_out[q]

    start(w_part(2))

    def w_forward():
        plus, minus = pl.ds(0, 512), pl.ds(512, 512)
        copies = []
        for a in (0, 1):
            copies += [
                send(wg.at[a, 1, plus], wg.at[a, 3, plus], wf_send, wf_recv.at[a], **{SEQ[a]: ring_at[a][2]}),
                send(wg.at[a, 2, minus], wg.at[a, 3, minus], wf_send, wf_recv.at[a], **{SEQ[a]: ring_at[a][1]}),
            ]
        return copies

    for g in range(4, 8):
        pair(g)
    for side in (0, 1):
        for j in range(4):
            ring_in[side, 0, j, :, 256 - 256 * side : 512 - 256 * side] = jnp.zeros((128, 256), BF16)

    def a_direct(p):
        copies = []
        for a in (0, 1):
            mine, all_rows = ag.at[a, pl.ds(p * 128, 32)], ag.at[a]
            axis, to = SEQ[1 - a], ring_at[1 - a]
            copies += [
                send(mine, all_rows.at[pl.ds(p * 128 + 32, 32)], a_send.at[0], a_recv.at[0, p], **{axis: to[2]}),
                send(mine, all_rows.at[pl.ds(p * 128 + 64, 32)], a_send.at[0], a_recv.at[0, p], **{axis: to[1]}),
            ]
        return copies

    def a_forward(p):
        copies = []
        for a in (0, 1):
            rows = ag.at[a]
            axis, to = SEQ[1 - a], ring_at[1 - a]
            copies += [
                send(rows.at[pl.ds(p * 128 + 32, 16)], rows.at[pl.ds(p * 128 + 96, 16)], a_send.at[1], a_recv.at[1, p], **{axis: to[2]}),
                send(rows.at[pl.ds(p * 128 + 80, 16)], rows.at[pl.ds(p * 128 + 112, 16)], a_send.at[1], a_recv.at[1, p], **{axis: to[1]}),
            ]
        return copies

    direct = {p: a_direct(p) for p in range(8)}
    passed = {p: a_forward(p) for p in range(8)}

    all_of(state.at[pl.ds(0, 240)], t_sem.at[1])

    def hidden(p):
        rows = pl.ds(pl.multiple_of(lax.rem(h + PIECES[p], 8) * 32, 32), 32)
        outside = jnp.dot(cc[rows, :], carried[...], preferred_element_type=F32)
        gated = inside[rows, :] + outside * grow[rows, :]
        inverse_rms = lax.rsqrt(jnp.mean(gated * gated, axis=1, keepdims=True) + epsilon)
        value = (gated * inverse_rms * gain[...]).astype(BF16)
        ag[0, p * 128 : p * 128 + 32, :] = value
        ag[1, p * 128 : p * 128 + 32, :] = value

    hidden(0)
    start(direct[0])
    hidden(1)
    start(direct[1])
    hidden(2)
    start(direct[2])
    for p in range(3, 8):
        hidden(p)
    for c in own_w:
        c.wait()

    def forward(p):
        all_of(ag.at[0, pl.ds(0, 128)], a_recv.at[0, p])
        start(passed[p])

    def arrived(p):
        all_of(ag.at[0, pl.ds(0, 64)], a_recv.at[1, p])

    def ring(stage, j, side):
        src, dst = ring_out.at[side, stage, j], ring_in.at[side, stage, j]
        return send(src, dst, r_send, r_recv.at[stage - 1, j], **{"head": sides[side]})

    def ring_first(j, side, group):
        low, size = ROWS[group]
        rows, half = pl.ds(low, size), pl.ds(side * 256, 256)
        return send(
            ring_out.at[side, 0, j, rows, half], ring_in.at[side, 0, j, rows, half],
            f_send, f_recv.at[j], **{"head": sides[side]},
        )

    rings = {(stage, j): [[ring(stage, j, side)] for side in (0, 1)] for stage in (1, 2, 3) for j in range(4)}
    for j in range(4):
        groups = (3,) if j == 3 else (0, 1, 2)
        rings[0, j] = [[ring_first(j, side, g) for g in groups] for side in (0, 1)]

    def first(j, group):
        low, size = ROWS[group]
        for a in (0, 1):
            part = jnp.dot(ag[a, low : low + size, :], wg[a, j], preferred_element_type=F32)
            ring_out[a, 0, j, low : low + size, a * 256 : a * 256 + 256] = part.astype(BF16)
        for side in (0, 1):
            start([rings[0, j][side][group % 3]])

    def middle(stage, j):
        p = 2 * stage - 1
        parts = [jnp.dot(ag[a, p * 128 : p * 128 + 256, :], wg[a, j], preferred_element_type=F32) for a in (0, 1)]
        if stage == 1:
            all_of(ring_in.at[0, 0, j], f_recv.at[j])
        else:
            all_of(ring_in.at[0, 0, pl.ds(0, 2)], r_recv.at[stage - 2, j])
        for side in (0, 1):
            for a in (0, 1):
                cols = slice(a * 256, a * 256 + 256)
                got = ring_in[side, stage - 1, j, :, cols].astype(F32)
                ring_out[side, stage, j, :, cols] = (parts[a][side * 128 : side * 128 + 128] + got).astype(BF16)
        start(rings[stage, j][0] + rings[stage, j][1])

    def final(j):
        parts = [jnp.dot(ag[a, 896:1024, :], wg[a, j], preferred_element_type=F32) for a in (0, 1)]
        all_of(ring_in.at[0, 0, pl.ds(0, 2)], r_recv.at[2, j])
        for a in (0, 1):
            half = slice(a * 256, a * 256 + 256)
            total = parts[a] + ring_in[0, 3, j, :, half].astype(F32) + ring_in[1, 3, j, :, half].astype(F32)
            done[a, j] = total.astype(BF16)
        copies = []
        for a in (0, 1):
            shard = ring_at[0][j] * 4 + y if a == 0 else x * 4 + ring_at[1][j]
            cols = pl.ds(pl.multiple_of(shard * 512 + a * 256, 256), 256)
            for r in (3, 1, 2, 0):
                axis = {SEQ[1 - a]: ring_at[1 - a][r]}
                copies.append(
                    send(done.at[a, j, pl.ds(r * 32, 32)], out.at[:, cols], o_sem.at[0], o_sem.at[1], section=1 - s, **axis)
                )
        start(copies)

    first(0, 0)
    for a in (0, 1):
        for side in (0, 1):
            all_of(wg.at[a, 1 + side], w_recv.at[a, side])
    first(1, 0)
    first(2, 0)
    forward(0)
    for j in range(3):
        first(j, 1)
    forward(1)
    forward(2)
    start(w_forward())
    arrived(0)
    for j in range(3):
        first(j, 2)
    start(direct[3])
    start(direct[4])
    arrived(1)
    arrived(2)
    for j in range(3):
        middle(1, j)
        if j > 0:
            forward(2 + j)
            start(direct[4 + j])
    for a in (0, 1):
        all_of(wg.at[a, 3], wf_recv.at[a])
    first(3, 3)
    arrived(3)
    arrived(4)
    for stage, j in ((2, 0), (2, 1), (1, 3), (2, 2)):
        middle(stage, j)
        if stage == 2 and j > 0:
            forward(4 + j)
    start(direct[7])
    arrived(5)
    arrived(6)
    for stage, j in ((3, 0), (2, 3), (3, 1), (3, 2), (3, 3)):
        middle(stage, j)
        if stage == 3 and j == 1:
            forward(7)
    arrived(7)
    for j in range(4):
        final(j)

    all_of(decay.at[pl.ds(0, 15)], d_sem.at[0])
    all_of(state.at[pl.ds(0, 240)], s_sem.at[0])
    all_of(state.at[pl.ds(0, 240)], t_sem.at[0])
    all_of(ag.at[0], w_send)
    all_of(ag.at[0, pl.ds(0, 512)], wf_send)
    all_of(ag.at[0, pl.ds(0, 256)], f_send)
    all_of(ag.at[0], a_send.at[0])
    all_of(ag.at[0, pl.ds(0, 512)], a_send.at[1])
    all_of(ring_out.at[:, pl.ds(1, 3)], r_send)
    all_of(done, o_sem.at[0])

    @pl.when(q < 15)
    def _():
        for c in halo:
            c.wait_send()

    all_of(out, o_sem.at[1])


def per_device(
    x_in, b_in, c_in, z_in, dt_raw, conv_x, conv_b, conv_c, a_rate, dt_bias, skip_d, norm_gain, out_weight
):
    dma = pltpu.SemaphoreType.DMA
    half = lambda *shape: pltpu.VMEM(shape, BF16)
    full = lambda *shape: pltpu.VMEM(shape, F32)
    anywhere = pl.BlockSpec(memory_space=pl.ANY)
    mixed = pl.pallas_call(
        mixer_kernel,
        out_shape=jax.ShapeDtypeStruct((32, 8192), BF16),
        in_specs=[anywhere] * 13,
        out_specs=anywhere,
        scratch_shapes=[
            half(256, 1024), half(256, 256), half(256, 256), half(256, 1024), full(16, 256),
            full(4, 1024), full(4, 256), full(4, 256), full(1, 16), full(1, 16), full(1, 16), full(1, 1024),
            half(16, 1024), half(16, 256), half(16, 256), full(264, 1024), full(264, 256), full(264, 256),
            half(256, 1024), half(256, 256), half(256, 256), half(256, 1024),
            full(16, 256), full(16, 256), full(8, 128), full(16, 8, 128),
            half(256, 1024), half(16, 16, 1024), half(16, 16, 1024), half(256, 1024),
            full(256, 256), full(256, 1024), full(256, 1024), full(256, 1024),
            half(2, 4, 1024, 256), half(2, 1024, 1024), half(2, 4, 4, 128, 512), half(2, 4, 4, 128, 512), half(2, 4, 128, 256),
            dma((12,)), dma((3,)), dma((3,)), dma((2,)), dma((2,)), dma((2,)),
            dma((2,)), dma, dma((2, 2)), dma, dma((2,)), dma, dma((4,)), dma((2,)), dma((2, 8)), dma, dma((3, 4)), dma((2,)),
        ],
        compiler_params=pltpu.CompilerParams(
            collective_id=0, has_side_effects=True, vmem_limit_bytes=56 * 2**20
        ),
    )(
        x_in[0], b_in[0], c_in[0], z_in[0], dt_raw[0], conv_x[0], conv_b[0], conv_c[0],
        a_rate, dt_bias, skip_d, norm_gain, out_weight[0],
    )
    return mixed[None]


def solution(mesh):
    finer = Mesh(
        mesh.devices.reshape(mesh.shape["section"], 4, 4, mesh.shape["head"]),
        ("section", "seq_0", "seq_1", "head"),
    )
    return jax.shard_map(
        per_device,
        mesh=finer,
        in_specs=(
            P("section", SEQ, "head"),
            P("section", SEQ, "head"),
            P("section", SEQ, "head"),
            P("section", SEQ, "head"),
            P("section", "head", SEQ),
            P("section", None, "head"),
            P("section", None, "head"),
            P("section", None, "head"),
            P("section", "head"),
            P("section", "head"),
            P("section", "head"),
            P("section", "head"),
            P("section", "head", SEQ),
        ),
        out_specs=P("section", SEQ_HEAD, None),
        check_vma=False,
    )
```

time: 99.9 us -> 88.7 us (0.89)
  Pallas kernels: 97.9 us -> 86.7 us
    pallas_call x1, Pallas kernels: 97.9 us -> 86.7 us  [per_device(): pl.pallas_call(mixer_kernel, out_shape=jax.ShapeDtypeStruct((32, 8192), B...]
where the time goes in v3:
time: 88.7 us; the launch traced here: 88.6 us
  Pallas kernels  86.7 us (98%)
  local copies, waits for them, and re-layouts  1.87 us (2%)
    pallas_call x1, Pallas kernels, per_device(): pl.pallas_call(mixer_kernel, out_shape=jax.ShapeDtypeStruct((32, 8192), B...  86.7 us
    unnamed x1, local copies, waits for them, and re-layouts  1.87 us

profile of v3, /device:TPU:1, one launch (start us, length us, event | category | flops | bytes accessed | tf_op | source)
XLA Modules:
  0.0 88.6 jit_solution(15786666830575083447)
XLA Ops:
  0.0 86.7 %shard_map.127 = bf16[32,8192]{1,0:T(8,128)(2,1)} custom-call(bf16[256,1024]{1,0:T(8,128)(2,1)} %bitcast.12, bf16[256,256]{1,0:T(8,128)(2,1)} %bitcast.14, bf16[256,256]{1,0:T(8,128)(2,1)} %bitcast.15, bf16[256,1024]{1,0:T(8,128)(2,1)} %bitcast.13, f32[16,256]{1,0:T(8,128)} %bitcast.16, f32[4,1024]{1,0:T(4,128)} %bitcast.17, f32[4,256]{1,0:T(4,128)} %bitcast.18, ...), custom_call_target="tpu_custom_call" | custom-call | tf_op jit(solution)/shard_map/pallas_call | solution.py:442
  86.7 1.9 %copy.15 = bf16[1,32,8192]{2,1,0:T(8,128)(2,1)} copy(bf16[1,32,8192]{2,1,0:T(8,128)(2,1)} %bitcast.10) | data formatting | bytes 1048576

commit v4 on v3

--- a/solution.py
+++ b/solution.py
@@ -12,11 +12,27 @@
 PIECES = (4, 3, 5, 2, 6, 1, 7, 0)
 OFFSETS = (0, 3, 1, 2)
 PEERS = tuple((dx, dy) for dx in (2, 1, 3, 0) for dy in (2, 1, 3, 0) if dx or dy)
-W_CUTS = (0, 336, 672, 1024)
-ROWS = ((0, 32), (32, 64), (96, 32), (0, 128))
+W_CUT = 672
+UNITS = ((0, None), (1, 0), (2, 0), (1, 1), (2, 1), (3, 0), (3, 1))
+ALL, NEAR, FAR, OWN, SIDE = (0, 128), (0, 96), (96, 32), (0, 32), (32, 64)
 F32 = jnp.float32
+ORDER = (
+    ("hd", 0), ("hd", 2), ("first", 0, OWN), ("first", 2, OWN), ("hd", 1), ("first", 1, OWN),
+    ("hd", 3), ("hd", 4), ("first", 2, SIDE), ("fw", 0), ("wb",), ("first", 0, SIDE),
+    ("first", 1, SIDE), ("fw", 1), ("fw", 2), ("wf", 0), ("mid", 1, 2, NEAR), ("mid", 1, 0, NEAR),
+    ("first", 0, FAR), ("first", 1, FAR), ("mid", 1, 1, NEAR), ("mid", 2, 2, NEAR), ("first", 2, FAR), ("fw", 3),
+    ("mid", 2, 0, NEAR), ("first", 4, ALL), ("mid", 2, 1, NEAR), ("fw", 4), ("first", 3, ALL), ("wf", 1),
+    ("mid", 1, 2, FAR), ("mid", 1, 0, FAR), ("hd", 6), ("mid", 1, 1, FAR), ("mid", 1, 4, ALL), ("first", 5, ALL),
+    ("mid", 1, 3, ALL), ("mid", 2, 2, FAR), ("mid", 2, 0, FAR), ("mid", 2, 1, FAR), ("hd", 5), ("first", 6, ALL),
+    ("mid", 1, 5, ALL), ("mid", 2, 3, ALL), ("fw", 5), ("mid", 2, 4, ALL), ("fw", 6), ("mid", 1, 6, ALL),
+    ("mid", 2, 5, ALL), ("mid", 3, 0, ALL), ("hd", 7), ("mid", 3, 1, ALL), ("mid", 2, 6, ALL), ("fw", 7),
+    ("mid", 3, 5, ALL), ("mid", 3, 2, ALL), ("mid", 3, 4, ALL), ("mid", 3, 3, ALL), ("mid", 3, 6, ALL), ("fin", 0),
+    ("fin", 4), ("fin", 2), ("fin", 1), ("fin", 5), ("fin", 3), ("fin", 6),
+)
 BF16 = jnp.bfloat16
 
+SPLIT = 2
+SPLIT_UNITS = 3
 epsilon = 1e-05
 
 
@@ -138,19 +154,18 @@
         for i, (u, v) in enumerate(peers)
     ])
 
-    def w_part(i):
-        n = W_CUTS[i + 1] - W_CUTS[i]
-        plus, minus = pl.ds(W_CUTS[i], n), pl.ds(1024 - W_CUTS[i + 1], n)
+    def w_direct(b, low, size, sems):
+        rows = pl.ds(low, size)
         copies = []
         for a in (0, 1):
-            cols = pl.ds(a * 256, 256)
-            copies += [
-                send(w.at[plus, cols], wg.at[a, 1, plus], w_send, w_recv.at[a, 0], **{SEQ[a]: ring_at[a][2]}),
-                send(w.at[minus, cols], wg.at[a, 2, minus], w_send, w_recv.at[a, 1], **{SEQ[a]: ring_at[a][1]}),
-            ]
+            for slot, to in ((1, 2), (2, 1)):
+                copies.append(send(
+                    w.at[rows, pl.ds(a * 256 + b * 128, 128)], wg.at[a, slot, rows, pl.ds(b * 128, 128)],
+                    sems[0], sems[1], **{SEQ[a]: ring_at[a][to]},
+                ))
         return copies
 
-    start(w_part(0))
+    start(w_direct(0, 0, W_CUT, (w_send, w_recv.at[0])))
 
     loaded("kb", "kx", "kc", "skip", "z", "gain")
     pad_x[8:264, :] = x_in[...].astype(F32)
@@ -188,7 +203,7 @@
         )
         for i, (u, v) in enumerate(peers)
     ])
-    start(w_part(1))
+    start(w_direct(0, W_CUT, 1024 - W_CUT, (w_send, w_recv.at[0])))
 
     conv_blocks(pad_c, conv_c, cc, (1, 2, 3))
     finish(2, halo_c, pad_c, conv_c, cc)
@@ -240,24 +255,24 @@
     ])
     carried[my_rows, :] = state_out[q]
 
-    start(w_part(2))
-
-    def w_forward():
-        plus, minus = pl.ds(0, 512), pl.ds(512, 512)
+    def w_forward(b):
+        cols = pl.ds(b * 128, 128)
         copies = []
         for a in (0, 1):
-            copies += [
-                send(wg.at[a, 1, plus], wg.at[a, 3, plus], wf_send, wf_recv.at[a], **{SEQ[a]: ring_at[a][2]}),
-                send(wg.at[a, 2, minus], wg.at[a, 3, minus], wf_send, wf_recv.at[a], **{SEQ[a]: ring_at[a][1]}),
-            ]
+            for slot, to, low in ((1, 2, 0), (2, 1, 512)):
+                at = (pl.ds(low, 512), cols)
+                copies.append(send(
+                    wg.at[(a, slot, *at)], wg.at[(a, 3, *at)], wf_send, wf_recv.at[b], **{SEQ[a]: ring_at[a][to]},
+                ))
         return copies
 
     for g in range(4, 8):
         pair(g)
     for side in (0, 1):
         for j in range(4):
-            ring_in[side, 0, j, :, 256 - 256 * side : 512 - 256 * side] = jnp.zeros((128, 256), BF16)
-
+            for b in (0, 1):
+                at = b * 256 + (1 - side) * 128
+                ring_in[side, 0, j, :, at : at + 128] = jnp.zeros((128, 128), BF16)
     def a_direct(p):
         copies = []
         for a in (0, 1):
@@ -294,124 +309,157 @@
         ag[0, p * 128 : p * 128 + 32, :] = value
         ag[1, p * 128 : p * 128 + 32, :] = value
 
-    hidden(0)
-    start(direct[0])
-    hidden(1)
-    start(direct[1])
-    hidden(2)
-    start(direct[2])
-    for p in range(3, 8):
-        hidden(p)
-    for c in own_w:
-        c.wait()
-
-    def forward(p):
-        all_of(ag.at[0, pl.ds(0, 128)], a_recv.at[0, p])
-        start(passed[p])
-
-    def arrived(p):
-        all_of(ag.at[0, pl.ds(0, 64)], a_recv.at[1, p])
-
-    def ring(stage, j, side):
-        src, dst = ring_out.at[side, stage, j], ring_in.at[side, stage, j]
-        return send(src, dst, r_send, r_recv.at[stage - 1, j], **{"head": sides[side]})
-
-    def ring_first(j, side, group):
-        low, size = ROWS[group]
-        rows, half = pl.ds(low, size), pl.ds(side * 256, 256)
-        return send(
-            ring_out.at[side, 0, j, rows, half], ring_in.at[side, 0, j, rows, half],
-            f_send, f_recv.at[j], **{"head": sides[side]},
-        )
-
-    rings = {(stage, j): [[ring(stage, j, side)] for side in (0, 1)] for stage in (1, 2, 3) for j in range(4)}
-    for j in range(4):
-        groups = (3,) if j == 3 else (0, 1, 2)
-        rings[0, j] = [[ring_first(j, side, g) for g in groups] for side in (0, 1)]
-
-    def first(j, group):
-        low, size = ROWS[group]
-        for a in (0, 1):
-            part = jnp.dot(ag[a, low : low + size, :], wg[a, j], preferred_element_type=F32)
-            ring_out[a, 0, j, low : low + size, a * 256 : a * 256 + 256] = part.astype(BF16)
+    seen = set()
+
+    def need(key):
+        if key in seen:
+            return
+        seen.add(key)
+        kind, index = key
+        if kind == "own":
+            for c in own_w:
+                c.wait()
+        if kind == "direct":
+            all_of(ag.at[0, pl.ds(0, 128)], a_recv.at[0, index])
+        if kind == "passed":
+            all_of(ag.at[0, pl.ds(0, 64)], a_recv.at[1, index])
+        if kind == "w":
+            all_of(ag.at[0, pl.ds(0, 512)], w_recv.at[index])
+        if kind == "wf":
+            all_of(ag.at[0, pl.ds(0, 256)], wf_recv.at[index])
+
+    def need_rows(p, group):
+        need(("direct", p))
+        if group in (ALL, FAR):
+            need(("passed", p))
+
+    def need_w(u):
+        j, b = UNITS[u]
+        need(("own", 0))
+        if j in (1, 2):
+            need(("w", b))
+        if j == 3:
+            need(("wf", b))
+
+    def unit_cols(u):
+        b = UNITS[u][1]
+        return (0, 512) if b is None else (b * 256, 256)
+
+    def halves(u):
+        b = UNITS[u][1]
+        return (0, 1) if b is None else (b,)
+
+    def products(low, size, u):
+        j, b = UNITS[u]
+        cols = slice(0, 256) if b is None else slice(b * 128, b * 128 + 128)
+        parts = []
+        for a in (0, 1):
+            part = jnp.dot(ag[a, low : low + size, :], wg[a, j, :, cols], preferred_element_type=F32)
+            parts.append({v: part[:, i * 128 : i * 128 + 128] for i, v in enumerate(halves(u))})
+        return parts
+
+    def first(u, group):
+        low, size = group
+        j = UNITS[u][0]
+        need_w(u)
+        if group != OWN:
+            need_rows(0, group)
+        parts = products(low, size, u)
+        copies = []
+        for a in (0, 1):
+            for b in halves(u):
+                at = b * 256 + a * 128
+                ring_out[a, 0, j, low : low + size, at : at + 128] = parts[a][b].astype(BF16)
+                rows, cols = pl.ds(low, size), pl.ds(at, 128)
+                copies.append(send(
+                    ring_out.at[a, 0, j, rows, cols], ring_in.at[a, 0, j, rows, cols],
+                    f_send, f_recv.at[u, int(group == FAR)], **{"head": sides[a]},
+                ))
+        start(copies)
+
+    def ring_wait(stage, u, group):
+        low, size = group
+        n = unit_cols(u)[1]
+        sem = (f_recv.at[u, int(group == FAR)] if stage == 0 else r_recv.at[stage - 1, u, int(group == FAR)])
+        if stage == 0:
+            all_of(ring_in.at[0, 0, 0, pl.ds(low, size), pl.ds(0, n)], sem)
+        else:
+            all_of(ring_in.at[0, 0, pl.ds(0, 2), pl.ds(low, size), pl.ds(0, n)], sem)
+
+    def middle(stage, u, group=ALL):
+        p = 2 * stage - 1
+        low, size = group
+        j = UNITS[u][0]
+        need_w(u)
+        need_rows(p, group)
+        need_rows(p + 1, group)
+        if group == ALL:
+            both = products(p * 128, 256, u)
+            parts = [[{b: both[a][b][side * 128 : side * 128 + 128] for b in halves(u)} for a in (0, 1)] for side in (0, 1)]
+        else:
+            parts = [products((p + side) * 128 + low, size, u) for side in (0, 1)]
+        for waited in ((NEAR, FAR) if group == ALL and split(stage - 1, u) else (group,)):
+            ring_wait(stage - 1, u, waited)
+        rows = slice(low, low + size)
         for side in (0, 1):
-            start([rings[0, j][side][group % 3]])
-
-    def middle(stage, j):
-        p = 2 * stage - 1
-        parts = [jnp.dot(ag[a, p * 128 : p * 128 + 256, :], wg[a, j], preferred_element_type=F32) for a in (0, 1)]
-        if stage == 1:
-            all_of(ring_in.at[0, 0, j], f_recv.at[j])
-        else:
-            all_of(ring_in.at[0, 0, pl.ds(0, 2)], r_recv.at[stage - 2, j])
-        for side in (0, 1):
-            for a in (0, 1):
-                cols = slice(a * 256, a * 256 + 256)
-                got = ring_in[side, stage - 1, j, :, cols].astype(F32)
-                ring_out[side, stage, j, :, cols] = (parts[a][side * 128 : side * 128 + 128] + got).astype(BF16)
-        start(rings[stage, j][0] + rings[stage, j][1])
-
-    def final(j):
-        parts = [jnp.dot(ag[a, 896:1024, :], wg[a, j], preferred_element_type=F32) for a in (0, 1)]
-        all_of(ring_in.at[0, 0, pl.ds(0, 2)], r_recv.at[2, j])
-        for a in (0, 1):
-            half = slice(a * 256, a * 256 + 256)
-            total = parts[a] + ring_in[0, 3, j, :, half].astype(F32) + ring_in[1, 3, j, :, half].astype(F32)
-            done[a, j] = total.astype(BF16)
+            for b in halves(u):
+                for a in (0, 1):
+                    cols = slice(b * 256 + a * 128, b * 256 + a * 128 + 128)
+                    got = ring_in[side, stage - 1, j, rows, cols].astype(F32)
+                    ring_out[side, stage, j, rows, cols] = (parts[side][a][b] + got).astype(BF16)
+        at = (pl.ds(low, size), pl.ds(*unit_cols(u)))
+        start([
+            send(
+                ring_out.at[(side, stage, j, *at)], ring_in.at[(side, stage, j, *at)],
+                r_send, r_recv.at[stage - 1, u, int(group == FAR)], **{"head": sides[side]},
+            )
+            for side in (0, 1)
+        ])
+
+    def split(stage, u):
+        return u < SPLIT_UNITS and stage <= SPLIT
+
+    def final(u):
+        j, b = UNITS[u]
+        need_w(u)
+        need_rows(7, ALL)
+        parts = products(896, 128, u)
+        for waited in ((NEAR, FAR) if split(3, u) else (ALL,)):
+            ring_wait(3, u, waited)
+        low, n = (0, 256) if b is None else (b * 128, 128)
         copies = []
         for a in (0, 1):
+            for v in halves(u):
+                at = v * 256 + a * 128
+                total = parts[a][v] + ring_in[0, 3, j, :, at : at + 128].astype(F32) + ring_in[1, 3, j, :, at : at + 128].astype(F32)
+                done[a, j, :, v * 128 : v * 128 + 128] = total.astype(BF16)
             shard = ring_at[0][j] * 4 + y if a == 0 else x * 4 + ring_at[1][j]
-            cols = pl.ds(pl.multiple_of(shard * 512 + a * 256, 256), 256)
+            cols = pl.ds(pl.multiple_of(shard * 512 + a * 256 + low, 128), n)
             for r in (3, 1, 2, 0):
                 axis = {SEQ[1 - a]: ring_at[1 - a][r]}
-                copies.append(
-                    send(done.at[a, j, pl.ds(r * 32, 32)], out.at[:, cols], o_sem.at[0], o_sem.at[1], section=1 - s, **axis)
-                )
+                copies.append(send(
+                    done.at[a, j, pl.ds(r * 32, 32), pl.ds(low, n)], out.at[:, cols], o_sem.at[0], o_sem.at[1], section=1 - s, **axis
+                ))
         start(copies)
 
-    first(0, 0)
-    for a in (0, 1):
-        for side in (0, 1):
-            all_of(wg.at[a, 1 + side], w_recv.at[a, side])
-    first(1, 0)
-    first(2, 0)
-    forward(0)
-    for j in range(3):
-        first(j, 1)
-    forward(1)
-    forward(2)
-    start(w_forward())
-    arrived(0)
-    for j in range(3):
-        first(j, 2)
-    start(direct[3])
-    start(direct[4])
-    arrived(1)
-    arrived(2)
-    for j in range(3):
-        middle(1, j)
-        if j > 0:
-            forward(2 + j)
-            start(direct[4 + j])
-    for a in (0, 1):
-        all_of(wg.at[a, 3], wf_recv.at[a])
-    first(3, 3)
-    arrived(3)
-    arrived(4)
-    for stage, j in ((2, 0), (2, 1), (1, 3), (2, 2)):
-        middle(stage, j)
-        if stage == 2 and j > 0:
-            forward(4 + j)
-    start(direct[7])
-    arrived(5)
-    arrived(6)
-    for stage, j in ((3, 0), (2, 3), (3, 1), (3, 2), (3, 3)):
-        middle(stage, j)
-        if stage == 3 and j == 1:
-            forward(7)
-    arrived(7)
-    for j in range(4):
-        final(j)
+    for op, *at in ORDER:
+        if op == "hd":
+            hidden(*at)
+            start(direct[at[0]])
+        if op == "fw":
+            need(("direct", *at))
+            start(passed[at[0]])
+        if op == "wf":
+            need(("w", *at))
+            start(w_forward(*at))
+        if op == "wb":
+            start(w_direct(1, 0, 1024, (w_send, w_recv.at[1])))
+        if op == "first":
+            first(*at)
+        if op == "mid":
+            middle(*at)
+        if op == "fin":
+            final(*at)
 
     all_of(decay.at[pl.ds(0, 15)], d_sem.at[0])
     all_of(state.at[pl.ds(0, 240)], s_sem.at[0])
@@ -441,9 +489,9 @@
     anywhere = pl.BlockSpec(memory_space=pl.ANY)
     mixed = pl.pallas_call(
         mixer_kernel,
-        out_shape=jax.ShapeDtypeStruct((32, 8192), BF16),
+        out_shape=pltpu.VMEM((32, 8192), BF16),
         in_specs=[anywhere] * 13,
-        out_specs=anywhere,
+        out_specs=pl.BlockSpec(memory_space=pltpu.VMEM),
         scratch_shapes=[
             half(256, 1024), half(256, 256), half(256, 256), half(256, 1024), full(16, 256),
             full(4, 1024), full(4, 256), full(4, 256), full(1, 16), full(1, 16), full(1, 16), full(1, 1024),
@@ -454,7 +502,7 @@
             full(256, 256), full(256, 1024), full(256, 1024), full(256, 1024),
             half(2, 4, 1024, 256), half(2, 1024, 1024), half(2, 4, 4, 128, 512), half(2, 4, 4, 128, 512), half(2, 4, 128, 256),
             dma((12,)), dma((3,)), dma((3,)), dma((2,)), dma((2,)), dma((2,)),
-            dma((2,)), dma, dma((2, 2)), dma, dma((2,)), dma, dma((4,)), dma((2,)), dma((2, 8)), dma, dma((3, 4)), dma((2,)),
+            dma((2,)), dma, dma((2,)), dma, dma((2,)), dma, dma((7, 2)), dma((2,)), dma((2, 8)), dma, dma((3, 7, 2)), dma((2,)),
         ],
         compiler_params=pltpu.CompilerParams(
             collective_id=0, has_side_effects=True, vmem_limit_bytes=56 * 2**20

time: 88.7 us -> 84.1 us (0.948)
  Pallas kernels: 86.7 us -> 83.2 us
  local copies, waits for them, and re-layouts: 1.87 us -> 0.8 us
    pallas_call x1, Pallas kernels: 86.7 us -> 83.2 us  [per_device(): pl.pallas_call(mixer_kernel, out_shape=pltpu.VMEM((32, 8192), BF16), in_s...]
    unnamed x1, local copies, waits for them, and re-layouts: 1.87 us -> 0.8 us
where the time goes in v4:
time: 84.1 us; the launch traced here: 84 us
  Pallas kernels  83.2 us (99%)
    pallas_call x1, Pallas kernels, per_device(): pl.pallas_call(mixer_kernel, out_shape=pltpu.VMEM((32, 8192), BF16), in_s...  83.2 us

profile of v4, /device:TPU:1, one launch (start us, length us, event | category | flops | bytes accessed | tf_op | source)
XLA Modules:
  0.0 84.0 jit_solution(2465591977352215531)
XLA Ops:
  0.0 83.2 %shard_map.127 = bf16[32,8192]{1,0:T(8,128)(2,1)S(1)} custom-call(bf16[256,1024]{1,0:T(8,128)(2,1)} %bitcast.12, bf16[256,256]{1,0:T(8,128)(2,1)} %bitcast.14, bf16[256,256]{1,0:T(8,128)(2,1)} %bitcast.15, bf16[256,1024]{1,0:T(8,128)(2,1)} %bitcast.13, f32[16,256]{1,0:T(8,128)} %bitcast.16, f32[4,1024]{1,0:T(4,128)} %bitcast.17, f32[4,256]{1,0:T(4,128)} %bitcast.18, ...), custom_call_target="tpu_custom_call" | custom-call | tf_op jit(solution)/shard_map/pallas_call | solution.py:490
  83.2 0.8 copy.15

commit v5 on v4

--- a/solution.py
+++ b/solution.py
@@ -14,25 +14,31 @@
 PEERS = tuple((dx, dy) for dx in (2, 1, 3, 0) for dy in (2, 1, 3, 0) if dx or dy)
 W_CUT = 672
 UNITS = ((0, None), (1, 0), (2, 0), (1, 1), (2, 1), (3, 0), (3, 1))
-ALL, NEAR, FAR, OWN, SIDE = (0, 128), (0, 96), (96, 32), (0, 32), (32, 64)
+ALL, FAR, OWN, SIDE = (0, 128), (96, 32), (0, 32), (32, 64)
+SLOT = {ALL: 0, OWN: 0, SIDE: 1, FAR: 2}
 F32 = jnp.float32
 ORDER = (
-    ("hd", 0), ("hd", 2), ("first", 0, OWN), ("first", 2, OWN), ("hd", 1), ("first", 1, OWN),
-    ("hd", 3), ("hd", 4), ("first", 2, SIDE), ("fw", 0), ("wb",), ("first", 0, SIDE),
-    ("first", 1, SIDE), ("fw", 1), ("fw", 2), ("wf", 0), ("mid", 1, 2, NEAR), ("mid", 1, 0, NEAR),
-    ("first", 0, FAR), ("first", 1, FAR), ("mid", 1, 1, NEAR), ("mid", 2, 2, NEAR), ("first", 2, FAR), ("fw", 3),
-    ("mid", 2, 0, NEAR), ("first", 4, ALL), ("mid", 2, 1, NEAR), ("fw", 4), ("first", 3, ALL), ("wf", 1),
-    ("mid", 1, 2, FAR), ("mid", 1, 0, FAR), ("hd", 6), ("mid", 1, 1, FAR), ("mid", 1, 4, ALL), ("first", 5, ALL),
-    ("mid", 1, 3, ALL), ("mid", 2, 2, FAR), ("mid", 2, 0, FAR), ("mid", 2, 1, FAR), ("hd", 5), ("first", 6, ALL),
-    ("mid", 1, 5, ALL), ("mid", 2, 3, ALL), ("fw", 5), ("mid", 2, 4, ALL), ("fw", 6), ("mid", 1, 6, ALL),
-    ("mid", 2, 5, ALL), ("mid", 3, 0, ALL), ("hd", 7), ("mid", 3, 1, ALL), ("mid", 2, 6, ALL), ("fw", 7),
-    ("mid", 3, 5, ALL), ("mid", 3, 2, ALL), ("mid", 3, 4, ALL), ("mid", 3, 3, ALL), ("mid", 3, 6, ALL), ("fin", 0),
-    ("fin", 4), ("fin", 2), ("fin", 1), ("fin", 5), ("fin", 3), ("fin", 6),
+    ("hd", 0), ("first", 1, OWN), ("hd", 4), ("first", 2, OWN), ("hd", 2), ("hd", 1),
+    ("first", 0, OWN), ("mid", 1, 1, OWN), ("fw", 0), ("wb",), ("mid", 1, 2, OWN), ("mid", 1, 0, OWN),
+    ("first", 1, SIDE), ("hd", 3), ("first", 2, SIDE), ("first", 0, SIDE), ("mid", 2, 1, OWN), ("mid", 2, 2, OWN),
+    ("mid", 2, 0, OWN), ("fw", 1), ("mid", 1, 1, SIDE), ("first", 1, FAR), ("mid", 1, 0, SIDE), ("mid", 1, 2, SIDE),
+    ("first", 0, FAR), ("first", 2, FAR), ("fw", 2), ("hd", 5), ("hd", 6), ("mid", 3, 2, OWN),
+    ("mid", 3, 1, OWN), ("mid", 3, 0, OWN), ("wf", 0), ("first", 4, ALL), ("first", 3, ALL), ("wf", 1),
+    ("mid", 2, 0, SIDE), ("mid", 2, 2, SIDE), ("mid", 1, 2, FAR), ("mid", 2, 1, SIDE), ("fw", 4), ("mid", 1, 0, FAR),
+    ("fw", 3), ("mid", 1, 3, ALL), ("mid", 1, 4, ALL), ("mid", 1, 1, FAR), ("first", 5, ALL), ("mid", 3, 0, SIDE),
+    ("fw", 5), ("mid", 3, 1, SIDE), ("first", 6, ALL), ("mid", 3, 2, SIDE), ("fw", 6), ("mid", 2, 0, FAR),
+    ("mid", 2, 2, FAR), ("mid", 2, 1, FAR), ("mid", 1, 5, ALL), ("mid", 1, 6, ALL), ("mid", 2, 3, ALL), ("hd", 7),
+    ("mid", 2, 4, ALL), ("mid", 2, 5, ALL), ("mid", 2, 6, ALL), ("mid", 3, 2, FAR), ("mid", 3, 1, FAR), ("fw", 7),
+    ("mid", 3, 0, FAR), ("mid", 3, 3, SIDE), ("mid", 3, 4, FAR), ("mid", 3, 3, FAR), ("mid", 3, 5, ALL), ("mid", 3, 6, FAR),
+    ("mid", 3, 4, SIDE), ("mid", 3, 6, SIDE), ("fin", 0, ALL), ("fin", 2, ALL), ("mid", 3, 6, OWN), ("mid", 3, 4, OWN),
+    ("mid", 3, 3, OWN), ("fin", 4, FAR), ("fin", 1, ALL), ("fin", 5, ALL), ("fin", 3, FAR), ("fin", 6, FAR),
+    ("fin", 3, SIDE), ("fin", 4, SIDE), ("fin", 6, SIDE), ("fin", 6, OWN), ("fin", 4, OWN), ("fin", 3, OWN),
 )
 BF16 = jnp.bfloat16
 
-SPLIT = 2
+SPLIT = 3
 SPLIT_UNITS = 3
+TAILS = (3, 4, 6)
 epsilon = 1e-05
 
 
@@ -109,6 +115,32 @@
         for c in copies:
             c.start()
 
+    loaded("b", "x", "c")
+    pl.semaphore_wait(barrier, len(greeted))
+
+    to_next = {"seq_0": lax.rem(x + lax.div(y + 1, 4), 4), "seq_1": lax.rem(y + 1, 4)}
+    halo = [
+        send(src.at[pl.ds(240, 16)], dst, h_send.at[i], h_recv.at[i], **to_next)
+        for i, (src, dst) in enumerate(((b_in, halo_b), (x_in, halo_x), (c_in, halo_c)))
+    ]
+
+    @pl.when(q < 15)
+    def _():
+        for c in halo:
+            c.start()
+
+    def w_direct(b, low, size, sems):
+        rows = pl.ds(low, size)
+        copies = []
+        for a in (0, 1):
+            for slot, to in ((1, 2), (2, 1)):
+                copies.append(send(
+                    w.at[rows, pl.ds(a * 256 + b * 128, 128)], wg.at[a, slot, rows, pl.ds(b * 128, 128)],
+                    sems[0], sems[1], **{SEQ[a]: ring_at[a][to]},
+                ))
+        return copies
+
+    start(w_direct(0, 0, W_CUT, (w_send, w_recv.at[0])))
     loaded("dt", "bias", "rate")
     row16 = lax.broadcasted_iota(jnp.int32, (16, 16), 0)
     col16 = lax.broadcasted_iota(jnp.int32, (16, 16), 1)
@@ -135,37 +167,10 @@
         decay_own[r : r + 1, :] = last[:, r * 128 : r * 128 + 128]
     decay[q] = decay_own[...]
 
-    loaded("b", "x", "c")
-    pl.semaphore_wait(barrier, len(greeted))
-
-    to_next = {"seq_0": lax.rem(x + lax.div(y + 1, 4), 4), "seq_1": lax.rem(y + 1, 4)}
-    halo = [
-        send(src.at[pl.ds(240, 16)], dst, h_send.at[i], h_recv.at[i], **to_next)
-        for i, (src, dst) in enumerate(((b_in, halo_b), (x_in, halo_x), (c_in, halo_c)))
-    ]
-
-    @pl.when(q < 15)
-    def _():
-        for c in halo:
-            c.start()
-
     start([
         send(decay_own, decay.at[q], d_sem.at[0], d_sem.at[1], seq_0=u, seq_1=v)
         for i, (u, v) in enumerate(peers)
     ])
-
-    def w_direct(b, low, size, sems):
-        rows = pl.ds(low, size)
-        copies = []
-        for a in (0, 1):
-            for slot, to in ((1, 2), (2, 1)):
-                copies.append(send(
-                    w.at[rows, pl.ds(a * 256 + b * 128, 128)], wg.at[a, slot, rows, pl.ds(b * 128, 128)],
-                    sems[0], sems[1], **{SEQ[a]: ring_at[a][to]},
-                ))
-        return copies
-
-    start(w_direct(0, 0, W_CUT, (w_send, w_recv.at[0])))
 
     loaded("kb", "kx", "kc", "skip", "z", "gain")
     pad_x[8:264, :] = x_in[...].astype(F32)
@@ -309,7 +314,7 @@
         ag[0, p * 128 : p * 128 + 32, :] = value
         ag[1, p * 128 : p * 128 + 32, :] = value
 
-    seen = set()
+    seen, ring_seen = set(), set()
 
     def need(key):
         if key in seen:
@@ -329,7 +334,8 @@
             all_of(ag.at[0, pl.ds(0, 256)], wf_recv.at[index])
 
     def need_rows(p, group):
-        need(("direct", p))
+        if group != OWN:
+            need(("direct", p))
         if group in (ALL, FAR):
             need(("passed", p))
 
@@ -373,14 +379,22 @@
                 rows, cols = pl.ds(low, size), pl.ds(at, 128)
                 copies.append(send(
                     ring_out.at[a, 0, j, rows, cols], ring_in.at[a, 0, j, rows, cols],
-                    f_send, f_recv.at[u, int(group == FAR)], **{"head": sides[a]},
+                    f_send, f_recv.at[u, SLOT[group]], **{"head": sides[a]},
                 ))
         start(copies)
+
+    def ring_need(stage, u, group):
+        groups = (OWN, SIDE, FAR) if split(stage, u) else (ALL,)
+        for waited in groups:
+            if group in (ALL, waited) or waited == ALL:
+                if (stage, u, waited) not in ring_seen:
+                    ring_seen.add((stage, u, waited))
+                    ring_wait(stage, u, waited)
 
     def ring_wait(stage, u, group):
         low, size = group
         n = unit_cols(u)[1]
-        sem = (f_recv.at[u, int(group == FAR)] if stage == 0 else r_recv.at[stage - 1, u, int(group == FAR)])
+        sem = (f_recv.at[u, SLOT[group]] if stage == 0 else r_recv.at[stage - 1, u, SLOT[group]])
         if stage == 0:
             all_of(ring_in.at[0, 0, 0, pl.ds(low, size), pl.ds(0, n)], sem)
         else:
@@ -398,8 +412,7 @@
             parts = [[{b: both[a][b][side * 128 : side * 128 + 128] for b in halves(u)} for a in (0, 1)] for side in (0, 1)]
         else:
             parts = [products((p + side) * 128 + low, size, u) for side in (0, 1)]
-        for waited in ((NEAR, FAR) if group == ALL and split(stage - 1, u) else (group,)):
-            ring_wait(stage - 1, u, waited)
+        ring_need(stage - 1, u, group)
         rows = slice(low, low + size)
         for side in (0, 1):
             for b in halves(u):
@@ -411,35 +424,39 @@
         start([
             send(
                 ring_out.at[(side, stage, j, *at)], ring_in.at[(side, stage, j, *at)],
-                r_send, r_recv.at[stage - 1, u, int(group == FAR)], **{"head": sides[side]},
+                r_send, r_recv.at[stage - 1, u, SLOT[group]], **{"head": sides[side]},
             )
             for side in (0, 1)
         ])
 
     def split(stage, u):
-        return u < SPLIT_UNITS and stage <= SPLIT
-
-    def final(u):
+        return (u < SPLIT_UNITS and stage <= SPLIT) or (u in TAILS and stage == 3)
+
+    def final(u, group):
         j, b = UNITS[u]
+        first_row, size = group
+        rows = slice(first_row, first_row + size)
         need_w(u)
-        need_rows(7, ALL)
-        parts = products(896, 128, u)
-        for waited in ((NEAR, FAR) if split(3, u) else (ALL,)):
-            ring_wait(3, u, waited)
+        need_rows(7, group)
+        parts = products(896 + first_row, size, u)
+        ring_need(3, u, group)
         low, n = (0, 256) if b is None else (b * 128, 128)
         copies = []
         for a in (0, 1):
             for v in halves(u):
                 at = v * 256 + a * 128
-                total = parts[a][v] + ring_in[0, 3, j, :, at : at + 128].astype(F32) + ring_in[1, 3, j, :, at : at + 128].astype(F32)
-                done[a, j, :, v * 128 : v * 128 + 128] = total.astype(BF16)
+                total = parts[a][v]
+                for side in (0, 1):
+                    total = total + ring_in[side, 3, j, rows, at : at + 128].astype(F32)
+                done[a, j, rows, v * 128 : v * 128 + 128] = total.astype(BF16)
             shard = ring_at[0][j] * 4 + y if a == 0 else x * 4 + ring_at[1][j]
             cols = pl.ds(pl.multiple_of(shard * 512 + a * 256 + low, 128), n)
             for r in (3, 1, 2, 0):
-                axis = {SEQ[1 - a]: ring_at[1 - a][r]}
-                copies.append(send(
-                    done.at[a, j, pl.ds(r * 32, 32), pl.ds(low, n)], out.at[:, cols], o_sem.at[0], o_sem.at[1], section=1 - s, **axis
-                ))
+                if first_row <= r * 32 < first_row + size:
+                    axis = {SEQ[1 - a]: ring_at[1 - a][r]}
+                    copies.append(send(
+                        done.at[a, j, pl.ds(r * 32, 32), pl.ds(low, n)], out.at[:, cols], o_sem.at[0], o_sem.at[1], section=1 - s, **axis
+                    ))
         start(copies)
 
     for op, *at in ORDER:
@@ -502,7 +519,7 @@
             full(256, 256), full(256, 1024), full(256, 1024), full(256, 1024),
             half(2, 4, 1024, 256), half(2, 1024, 1024), half(2, 4, 4, 128, 512), half(2, 4, 4, 128, 512), half(2, 4, 128, 256),
             dma((12,)), dma((3,)), dma((3,)), dma((2,)), dma((2,)), dma((2,)),
-            dma((2,)), dma, dma((2,)), dma, dma((2,)), dma, dma((7, 2)), dma((2,)), dma((2, 8)), dma, dma((3, 7, 2)), dma((2,)),
+            dma((2,)), dma, dma((2,)), dma, dma((2,)), dma, dma((7, 3)), dma((2,)), dma((2, 8)), dma, dma((3, 7, 3)), dma((2,)),
         ],
         compiler_params=pltpu.CompilerParams(
             collective_id=0, has_side_effects=True, vmem_limit_bytes=56 * 2**20

time: 84.1 us -> 82.4 us (0.980)
  Pallas kernels: 83.2 us -> 81.5 us
    pallas_call x1, Pallas kernels: 83.2 us -> 81.5 us  [per_device(): pl.pallas_call(mixer_kernel, out_shape=pltpu.VMEM((32, 8192), BF16), in_s...]
where the time goes in v5:
time: 82.4 us; the launch traced here: 82.3 us
  Pallas kernels  81.5 us (99%)
    pallas_call x1, Pallas kernels, per_device(): pl.pallas_call(mixer_kernel, out_shape=pltpu.VMEM((32, 8192), BF16), in_s...  81.5 us

profile of v5, /device:TPU:1, one launch (start us, length us, event | category | flops | bytes accessed | tf_op | source)
XLA Modules:
  0.0 82.3 jit_solution(11249252795004786459)
XLA Ops:
  0.0 81.5 %shard_map.127 = bf16[32,8192]{1,0:T(8,128)(2,1)S(1)} custom-call(bf16[256,1024]{1,0:T(8,128)(2,1)} %bitcast.12, bf16[256,256]{1,0:T(8,128)(2,1)} %bitcast.14, bf16[256,256]{1,0:T(8,128)(2,1)} %bitcast.15, bf16[256,1024]{1,0:T(8,128)(2,1)} %bitcast.13, f32[16,256]{1,0:T(8,128)} %bitcast.16, f32[4,1024]{1,0:T(4,128)} %bitcast.17, f32[4,256]{1,0:T(4,128)} %bitcast.18, ...), custom_call_target="tpu_custom_call" | custom-call | tf_op jit(solution)/shard_map/pallas_call | solution.py:507
  81.5 0.8 copy.15

commit v6 on v5

--- a/solution.py
+++ b/solution.py
@@ -11,28 +11,31 @@
 MESH = pl.DeviceIdType.MESH
 PIECES = (4, 3, 5, 2, 6, 1, 7, 0)
 OFFSETS = (0, 3, 1, 2)
-PEERS = tuple((dx, dy) for dx in (2, 1, 3, 0) for dy in (2, 1, 3, 0) if dx or dy)
+PEERS = (
+    (2, 2), (1, 2), (3, 2), (2, 1), (2, 3), (0, 2), (2, 0), (1, 1), (3, 3), (1, 3), (3, 1), (0, 1), (3, 0), (0, 3), (1, 0),
+)
 W_CUT = 672
 UNITS = ((0, None), (1, 0), (2, 0), (1, 1), (2, 1), (3, 0), (3, 1))
 ALL, FAR, OWN, SIDE = (0, 128), (96, 32), (0, 32), (32, 64)
 SLOT = {ALL: 0, OWN: 0, SIDE: 1, FAR: 2}
 F32 = jnp.float32
 ORDER = (
-    ("hd", 0), ("first", 1, OWN), ("hd", 4), ("first", 2, OWN), ("hd", 2), ("hd", 1),
-    ("first", 0, OWN), ("mid", 1, 1, OWN), ("fw", 0), ("wb",), ("mid", 1, 2, OWN), ("mid", 1, 0, OWN),
-    ("first", 1, SIDE), ("hd", 3), ("first", 2, SIDE), ("first", 0, SIDE), ("mid", 2, 1, OWN), ("mid", 2, 2, OWN),
-    ("mid", 2, 0, OWN), ("fw", 1), ("mid", 1, 1, SIDE), ("first", 1, FAR), ("mid", 1, 0, SIDE), ("mid", 1, 2, SIDE),
-    ("first", 0, FAR), ("first", 2, FAR), ("fw", 2), ("hd", 5), ("hd", 6), ("mid", 3, 2, OWN),
-    ("mid", 3, 1, OWN), ("mid", 3, 0, OWN), ("wf", 0), ("first", 4, ALL), ("first", 3, ALL), ("wf", 1),
-    ("mid", 2, 0, SIDE), ("mid", 2, 2, SIDE), ("mid", 1, 2, FAR), ("mid", 2, 1, SIDE), ("fw", 4), ("mid", 1, 0, FAR),
-    ("fw", 3), ("mid", 1, 3, ALL), ("mid", 1, 4, ALL), ("mid", 1, 1, FAR), ("first", 5, ALL), ("mid", 3, 0, SIDE),
-    ("fw", 5), ("mid", 3, 1, SIDE), ("first", 6, ALL), ("mid", 3, 2, SIDE), ("fw", 6), ("mid", 2, 0, FAR),
-    ("mid", 2, 2, FAR), ("mid", 2, 1, FAR), ("mid", 1, 5, ALL), ("mid", 1, 6, ALL), ("mid", 2, 3, ALL), ("hd", 7),
-    ("mid", 2, 4, ALL), ("mid", 2, 5, ALL), ("mid", 2, 6, ALL), ("mid", 3, 2, FAR), ("mid", 3, 1, FAR), ("fw", 7),
-    ("mid", 3, 0, FAR), ("mid", 3, 3, SIDE), ("mid", 3, 4, FAR), ("mid", 3, 3, FAR), ("mid", 3, 5, ALL), ("mid", 3, 6, FAR),
-    ("mid", 3, 4, SIDE), ("mid", 3, 6, SIDE), ("fin", 0, ALL), ("fin", 2, ALL), ("mid", 3, 6, OWN), ("mid", 3, 4, OWN),
-    ("mid", 3, 3, OWN), ("fin", 4, FAR), ("fin", 1, ALL), ("fin", 5, ALL), ("fin", 3, FAR), ("fin", 6, FAR),
-    ("fin", 3, SIDE), ("fin", 4, SIDE), ("fin", 6, SIDE), ("fin", 6, OWN), ("fin", 4, OWN), ("fin", 3, OWN),
+    ("wb", 2), ("hd", 0), ("first", 2, OWN), ("hd", 1), ("first", 0, OWN), ("hd", 2),
+    ("first", 1, OWN), ("wb", 0), ("mid", 1, 2, OWN), ("mid", 1, 0, OWN), ("mid", 1, 1, OWN), ("first", 0, SIDE),
+    ("first", 1, SIDE), ("fw", 0), ("wb", 3), ("wb", 1), ("hd", 4), ("hd", 3),
+    ("first", 2, SIDE), ("mid", 2, 2, OWN), ("mid", 2, 0, OWN), ("mid", 2, 1, OWN), ("fw", 1), ("fw", 2),
+    ("mid", 1, 0, SIDE), ("wf", 0), ("mid", 1, 1, SIDE), ("hd", 6), ("hd", 5), ("first", 2, FAR),
+    ("first", 1, FAR), ("mid", 3, 2, OWN), ("mid", 1, 2, SIDE), ("mid", 3, 0, OWN), ("first", 4, ALL), ("first", 3, ALL),
+    ("mid", 3, 1, OWN), ("wf", 1), ("first", 0, FAR), ("mid", 2, 0, SIDE), ("fw", 4), ("mid", 2, 1, SIDE),
+    ("fw", 3), ("mid", 2, 2, SIDE), ("mid", 1, 4, ALL), ("mid", 1, 1, FAR), ("first", 5, ALL), ("mid", 1, 0, FAR),
+    ("mid", 1, 3, ALL), ("mid", 3, 2, SIDE), ("mid", 3, 0, SIDE), ("hd", 7), ("fw", 5), ("mid", 1, 2, FAR),
+    ("first", 6, ALL), ("fw", 6), ("mid", 1, 5, ALL), ("mid", 2, 4, ALL), ("mid", 2, 1, FAR), ("mid", 2, 0, FAR),
+    ("mid", 2, 2, FAR), ("mid", 1, 6, ALL), ("mid", 2, 5, ALL), ("mid", 2, 3, ALL), ("mid", 3, 4, FAR), ("fw", 7),
+    ("mid", 3, 2, FAR), ("mid", 3, 1, FAR), ("mid", 2, 6, ALL), ("mid", 3, 5, ALL), ("mid", 3, 0, FAR), ("mid", 3, 1, SIDE),
+    ("fin", 2, ALL), ("fin", 4, FAR), ("mid", 3, 3, SIDE), ("mid", 3, 3, FAR), ("mid", 3, 6, FAR), ("mid", 3, 6, SIDE),
+    ("mid", 3, 4, SIDE), ("mid", 3, 6, OWN), ("mid", 3, 3, OWN), ("fin", 0, ALL), ("mid", 3, 4, OWN), ("fin", 1, ALL),
+    ("fin", 5, ALL), ("fin", 3, FAR), ("fin", 3, SIDE), ("fin", 6, FAR), ("fin", 6, SIDE), ("fin", 4, SIDE),
+    ("fin", 6, OWN), ("fin", 3, OWN), ("fin", 4, OWN),
 )
 BF16 = jnp.bfloat16
 
@@ -470,7 +473,7 @@
             need(("w", *at))
             start(w_forward(*at))
         if op == "wb":
-            start(w_direct(1, 0, 1024, (w_send, w_recv.at[1])))
+            start(w_direct(1, at[0] * 256, 256, (w_send, w_recv.at[1])))
         if op == "first":
             first(*at)
         if op == "mid":

time: 82.4 us -> 81.8 us (level)
  no operation moved by 1% of the time
where the time goes in v6:
time: 81.8 us; the launch traced here: 81.7 us
  Pallas kernels  80.9 us (99%)
    pallas_call x1, Pallas kernels, per_device(): pl.pallas_call(mixer_kernel, out_shape=pltpu.VMEM((32, 8192), BF16), in_s...  80.9 us

profile of v6, /device:TPU:1, one launch (start us, length us, event | category | flops | bytes accessed | tf_op | source)
XLA Modules:
  0.0 81.7 jit_solution(17815625525017047733)
XLA Ops:
  0.0 80.9 %shard_map.127 = bf16[32,8192]{1,0:T(8,128)(2,1)S(1)} custom-call(bf16[256,1024]{1,0:T(8,128)(2,1)} %bitcast.12, bf16[256,256]{1,0:T(8,128)(2,1)} %bitcast.14, bf16[256,256]{1,0:T(8,128)(2,1)} %bitcast.15, bf16[256,1024]{1,0:T(8,128)(2,1)} %bitcast.13, f32[16,256]{1,0:T(8,128)} %bitcast.16, f32[4,1024]{1,0:T(4,128)} %bitcast.17, f32[4,256]{1,0:T(4,128)} %bitcast.18, ...), custom_call_target="tpu_custom_call" | custom-call | tf_op jit(solution)/shard_map/pallas_call | solution.py:510
  80.9 0.8 copy.15

commit v7 on v6

--- a/solution.py
+++ b/solution.py
@@ -123,7 +123,7 @@
 
     to_next = {"seq_0": lax.rem(x + lax.div(y + 1, 4), 4), "seq_1": lax.rem(y + 1, 4)}
     halo = [
-        send(src.at[pl.ds(240, 16)], dst, h_send.at[i], h_recv.at[i], **to_next)
+        send(src.at[pl.ds(248, 8)], dst, h_send.at[i], h_recv.at[i], **to_next)
         for i, (src, dst) in enumerate(((b_in, halo_b), (x_in, halo_x), (c_in, halo_c)))
     ]
 
@@ -187,7 +187,7 @@
         @pl.when(q > 0)
         def _():
             halo[i].wait_recv()
-            padded[0:8, :] = halo_ref[...].astype(F32)[8:16]
+            padded[0:8, :] = halo_ref[...].astype(F32)
 
         @pl.when(q == 0)
         def _():
@@ -515,7 +515,7 @@
         scratch_shapes=[
             half(256, 1024), half(256, 256), half(256, 256), half(256, 1024), full(16, 256),
             full(4, 1024), full(4, 256), full(4, 256), full(1, 16), full(1, 16), full(1, 16), full(1, 1024),
-            half(16, 1024), half(16, 256), half(16, 256), full(264, 1024), full(264, 256), full(264, 256),
+            half(8, 1024), half(8, 256), half(8, 256), full(264, 1024), full(264, 256), full(264, 256),
             half(256, 1024), half(256, 256), half(256, 256), half(256, 1024),
             full(16, 256), full(16, 256), full(8, 128), full(16, 8, 128),
             half(256, 1024), half(16, 16, 1024), half(16, 16, 1024), half(256, 1024),

time: 81.8 us -> 81.7 us (level)
  no operation moved by 1% of the time
where the time goes in v7:
time: 81.7 us; the launch traced here: 81.6 us
  Pallas kernels  80.8 us (99%)
    pallas_call x1, Pallas kernels, per_device(): pl.pallas_call(mixer_kernel, out_shape=pltpu.VMEM((32, 8192), BF16), in_s...  80.8 us

profile of v7, /device:TPU:1, one launch (start us, length us, event | category | flops | bytes accessed | tf_op | source)
XLA Modules:
  0.0 81.6 jit_solution(9353670562406553778)
XLA Ops:
  0.0 80.8 %shard_map.127 = bf16[32,8192]{1,0:T(8,128)(2,1)S(1)} custom-call(bf16[256,1024]{1,0:T(8,128)(2,1)} %bitcast.12, bf16[256,256]{1,0:T(8,128)(2,1)} %bitcast.14, bf16[256,256]{1,0:T(8,128)(2,1)} %bitcast.15, bf16[256,1024]{1,0:T(8,128)(2,1)} %bitcast.13, f32[16,256]{1,0:T(8,128)} %bitcast.16, f32[4,1024]{1,0:T(4,128)} %bitcast.17, f32[4,256]{1,0:T(4,128)} %bitcast.18, ...), custom_call_target="tpu_custom_call" | custom-call | tf_op jit(solution)/shard_map/pallas_call | solution.py:510
  80.8 0.8 copy.15
